TPU v7x, 32 devices: a whole 2x2x4 slice. The times are simulated.
32 devices in a mesh: facet: 4 (over y, x), col: 8 (over z, core).
Axes of the slice: x: 2, y: 2, z: 4, core: 2. Of those that a mesh axis runs over, the one named last changes fastest.
Arguments:
- facets: bfloat16 [4, 2, 768, 768], P('facet', None, 'col'), may hold values from -6 to 6
- col_offsets: int32 [8], replicated, may hold values from 0 to 767
- sub_rows: int32 [4, 8], P(None, 'col'), may hold values from 0 to 767
- facet_offsets: int32 [4, 2], replicated, may hold values from 0 to 320
- vis_pos: int32 [4, 8, 2, 256], P('facet', 'col'), may hold values from 0 to 1535
- observed: float32 [4, 8, 2, 256], P('facet', 'col'), may hold values from -6 to 6
Outputs:
- predicted: float32 [4, 8, 2, 256], P('facet', 'col')
- facet_update: float32 [4, 2, 768, 768], P('facet', None, 'col')
All inputs are finite; a program needn't handle non-finite values.
Results may differ from a plain program's by a relative error of at most 0.0085.
Values may be sent and summed in bfloat16 or wider, within the bound.
A program may use at most 64 MiB of HBM per device.

v0:
```python
import functools
import math

import jax
import jax.numpy as jnp
from jax import lax
from jax.experimental import pallas as pl
from jax.experimental.pallas import tpu as pltpu
from jax.sharding import PartitionSpec as P

M = 64
SUB = 384
FINE = 1536
YN = 768
MARGIN = 8192
MESH = pl.DeviceIdType.MESH
F32 = jnp.float32
BF16 = jnp.bfloat16


def cis(product, modulus, direction):
    turns = jnp.floor(product * (1.0 / modulus) + 0.5)
    half = (product - turns * modulus) * (direction * math.pi / modulus)
    z = half * half
    s = half * (1.0 + z * (-1 / 6 + z * (1 / 120 + z * (-1 / 5040 + z * (1 / 362880 + z * (-1 / 39916800))))))
    c = 1.0 + z * (-1 / 2 + z * (1 / 24 + z * (-1 / 720 + z * (1 / 40320 + z * (-1 / 3628800 + z * (1 / 479001600))))))
    return 1.0 - 2.0 * s * s, 2.0 * s * c


def iota(shape, axis):
    return lax.broadcasted_iota(jnp.int32, shape, axis).astype(F32)


def dot(left, right, dims):
    return lax.dot_general(left, right, (dims, ((), ())), preferred_element_type=F32)


NN = ((1,), (0,))
NT = ((1,), (1,))
TN = ((0,), (0,))


def kernel(
    n_facet,
    n_col,
    facets_hbm,
    col_offsets_hbm,
    sub_rows_hbm,
    facet_offsets_hbm,
    vis_pos_hbm,
    observed_hbm,
    predicted,
    update,
    facet_buf,
    col_offsets,
    sub_rows,
    facet_offsets,
    vis_pos,
    observed,
    base,
    turn,
    wall,
    subt,
    subt_t,
    u_tab,
    v_tab,
    strip_out,
    strip_in,
    contrib_out,
    contrib_in,
    back_out,
    back_in,
    delta_out,
    delta_in,
    load_sem,
    col_send,
    col_recv,
    facet_send,
    facet_recv,
):
    my_f = lax.axis_index("facet")
    my_c = lax.axis_index("col")
    n_rows = facet_buf.shape[1]
    n_vis = vis_pos.shape[3]

    loads = [
        pltpu.make_async_copy(source, held, load_sem.at[i])
        for i, (source, held) in enumerate(
            (
                (col_offsets_hbm, col_offsets),
                (sub_rows_hbm, sub_rows),
                (facets_hbm.at[0], facet_buf),
                (facet_offsets_hbm, facet_offsets),
                (vis_pos_hbm, vis_pos),
                (observed_hbm, observed),
            )
        )
    ]
    for load in loads:
        load.start()
    barrier = pltpu.get_barrier_semaphore()
    n_pair = n_col // 2
    my_pair, my_core = my_c // 2, lax.rem(my_c, 2)
    side = my_pair // (n_pair // 2)
    mirrored = my_pair + side * (n_pair - 1 - 2 * my_pair)
    pair_order = []
    for place in range(n_pair - 1, 0, -1):
        target = place - (mirrored + n_pair - place) // n_pair
        pair_order.append(target + side * (n_pair - 1 - 2 * target))
    pair_order.append(my_pair)
    col_order = []
    for pair in pair_order:
        col_order += [2 * pair + 1 - my_core, 2 * pair + my_core]
    facet_order = [lax.rem(my_f + 1 + i, n_facet) for i in range(n_facet)]
    for c in col_order[:-1]:
        pl.semaphore_signal(barrier, inc=1, device_id=(my_f, c), device_id_type=MESH)
    for f in facet_order[:-1]:
        pl.semaphore_signal(barrier, inc=1, device_id=(f, my_c), device_id_type=MESH)

    def col_copy(phase, out, into, slot_out, slot_in, target):
        return pltpu.make_async_remote_copy(
            src_ref=out.at[slot_out],
            dst_ref=into.at[slot_in],
            send_sem=col_send.at[phase, slot_out],
            recv_sem=col_recv.at[phase, slot_in],
            device_id=(my_f, target),
            device_id_type=MESH,
        )

    def facet_copy(phase, out, into, slot_out, slot_in, target):
        return pltpu.make_async_remote_copy(
            src_ref=out.at[slot_out],
            dst_ref=into.at[slot_in],
            send_sem=facet_send.at[phase, slot_out],
            recv_sem=facet_recv.at[phase, slot_in],
            device_id=(target, my_c),
            device_id_type=MESH,
        )

    base_re, base_im = cis(iota((M, YN), 0) * iota((M, YN), 1), YN, -1.0)
    inv_root = 1.0 / math.sqrt(YN)
    base[0] = base_re * inv_root
    base[1] = base_im * inv_root
    along = iota((1, YN), 1)
    loads[0].wait()
    loads[1].wait()
    for c in range(n_col):
        turn[0, pl.ds(c, 1)] = along * col_offsets[c].astype(F32)
    for s in range(n_facet):
        turn[0, pl.ds(n_col + s, 1)] = along * sub_rows[0, s].astype(F32)
    turn_re, turn_im = cis(turn[0], YN, -1.0)
    turn[0] = turn_re
    turn[1] = turn_im

    def table(into, row, slot):
        re, im = turn[0, pl.ds(row, 1)], turn[1, pl.ds(row, 1)]
        into[slot, :M] = (base[0] * re - base[1] * im).astype(BF16)
        into[slot, M:] = (base[0] * im + base[1] * re).astype(BF16)

    lane = lax.broadcasted_iota(jnp.int32, (1, 2 * M), 1)
    minus_plus = jnp.where(lane < M, -1.0, 1.0)

    def swapped(value):
        return pltpu.roll(value, M, 1)

    loads[2].wait()
    both = facet_buf[...]
    if n_rows % 16:
        both = both.astype(F32).reshape(2 * n_rows, YN).astype(BF16)
    else:
        both = both.reshape(2 * n_rows, YN)
    early = n_col - 1
    for i, c in enumerate(col_order):
        table(wall, c, c)
        prod = dot(both, wall[c], NT)
        part = (prod[:n_rows] + minus_plus * swapped(prod[n_rows:])).astype(BF16)
        if i < n_col - 1:
            strip_out[c] = part
        else:
            strip_in[c] = part
        if i == early - 1:
            pl.semaphore_wait(barrier, n_col - 1 + n_facet - 1)
            for ready in col_order[:early]:
                col_copy(0, strip_out, strip_in, ready, my_c, ready).start()
        elif early <= i < n_col - 1:
            col_copy(0, strip_out, strip_in, c, my_c, c).start()

    for s in range(n_facet):
        table(subt, n_col + s, s)
    for load in loads[3:]:
        load.wait()
    for tab, which in ((u_tab, 0), (v_tab, 1)):
        point = vis_pos[0, 0, pl.ds(which, 1)].astype(F32)
        low_re, low_im = cis(iota((M, n_vis), 0) * point, FINE, 1.0)
        low_re = low_re * (1.0 / math.sqrt(SUB))
        low_im = low_im * (1.0 / math.sqrt(SUB))
        for f in range(n_facet):
            high_re, high_im = cis(point * facet_offsets[which, f].astype(F32), FINE, 1.0)
            tab[f, :M] = (low_re * high_re - low_im * high_im).astype(tab.dtype)
            tab[f, M:] = (low_re * high_im + low_im * high_re).astype(tab.dtype)
    for s in range(n_facet):
        subt_t[:, 2 * M * s : 2 * M * (s + 1)] = subt[s].T

    for c in col_order[:-1]:
        col_copy(0, strip_out, strip_in, c, c, c).wait_recv()
    strip = strip_in[...]
    if n_rows % 16:
        strip = strip.astype(F32).reshape(YN, 2 * M).astype(BF16)
    else:
        strip = strip.reshape(YN, 2 * M)
    for i, s in enumerate(facet_order):
        prod = dot(subt[s], strip, NN)
        part = (prod[:M] + minus_plus * swapped(prod[M:])).astype(BF16)
        if i < n_facet - 1:
            contrib_out[s] = part
            facet_copy(0, contrib_out, contrib_in, s, my_f, s).start()
        else:
            contrib_in[s] = part

    pred_re = jnp.zeros((M, n_vis), F32)
    pred_im = jnp.zeros((M, n_vis), F32)
    for i in range(n_facet):
        f = facet_order[n_facet - 1 - i]
        if i > 0:
            facet_copy(0, contrib_out, contrib_in, f, f, f).wait_recv()
        with_re = dot(contrib_in[f], u_tab[f, :M], TN)
        with_im = dot(contrib_in[f], u_tab[f, M:], TN)
        rows_re = with_re[:M] - with_im[M:]
        rows_im = with_im[:M] + with_re[M:]
        v_re, v_im = v_tab[f, :M], v_tab[f, M:]
        pred_re += rows_re * v_re - rows_im * v_im
        pred_im += rows_re * v_im + rows_im * v_re
    pred_re = jnp.sum(pred_re, axis=0, keepdims=True)
    pred_im = jnp.sum(pred_im, axis=0, keepdims=True)
    predicted[0, 0, pl.ds(0, 1)] = pred_re
    predicted[0, 0, pl.ds(1, 1)] = pred_im
    weight = SUB / math.sqrt(n_vis)
    diff_re = pred_re - observed[0, 0, pl.ds(0, 1)]
    diff_im = pred_im - observed[0, 0, pl.ds(1, 1)]
    for i, f in enumerate(facet_order):
        v_re, v_im = v_tab[f, :M], v_tab[f, M:]
        wgt_re = ((diff_re * v_re + diff_im * v_im) * weight).astype(BF16)
        wgt_im = ((diff_im * v_re - diff_re * v_im) * weight).astype(BF16)
        prod = dot(u_tab[f], jnp.concatenate([wgt_re, wgt_im], axis=0), NT)
        part = (prod[:M] - minus_plus * swapped(prod[M:])).astype(BF16)
        if i < n_facet - 1:
            back_out[f] = part
            facet_copy(1, back_out, back_in, f, my_f, f).start()
        else:
            back_in[f] = part

    for s in facet_order[:-1]:
        facet_copy(1, back_out, back_in, s, s, s).wait_recv()
    stacked = []
    for s in range(n_facet):
        block = back_in[s]
        stacked += [block, (-minus_plus * swapped(block.astype(F32))).astype(BF16)]
    back_scale = math.sqrt(YN / (M * n_facet))
    stacked = jnp.concatenate(stacked, axis=0)
    for i, pair in enumerate(pair_order):
        start = pl.multiple_of(pair * (2 * n_rows), 2 * n_rows)
        delta = dot(subt_t[pl.ds(start, 2 * n_rows)], stacked, NN) * back_scale
        delta_out[pl.ds(2 * pair, 2)] = delta.reshape(2, n_rows, 2 * M).astype(BF16)
        for c in col_order[2 * i : 2 * i + 2]:
            if c is not col_order[-1]:
                col_copy(1, delta_out, delta_in, c, my_c, c).start()
    delta_in[my_c] = delta_out[my_c]

    up_scale = math.sqrt(YN / (M * n_col))
    for i in reversed(range(n_pair)):
        for c in col_order[2 * i : 2 * i + 2]:
            if c is not col_order[-1]:
                col_copy(1, delta_out, delta_in, c, c, c).wait_recv()
        pair = pair_order[i]
        blocks = [delta_in[2 * pair + core] for core in range(2)]
        turned = [(-minus_plus * swapped(block.astype(F32))).astype(BF16) for block in blocks]
        walls = wall[pl.ds(2 * pair, 2)].reshape(4 * M, YN)
        for part, sides in enumerate((blocks, turned)):
            term = dot(jnp.concatenate(sides, axis=1), walls, NN)
            if i < n_pair - 1:
                term += update[0, part]
            update[0, part] = term * up_scale if i == 0 else term

    for c in col_order[:-1]:
        col_copy(0, strip_out, strip_in, c, c, c).wait_send()
        col_copy(1, delta_out, delta_in, c, c, c).wait_send()
    for f in facet_order[:-1]:
        facet_copy(0, contrib_out, contrib_in, f, f, f).wait_send()
        facet_copy(1, back_out, back_in, f, f, f).wait_send()


def deliver_kernel(predicted, update, predicted_hbm, update_hbm, sems):
    copies = [
        pltpu.make_async_copy(update, update_hbm, sems.at[0]),
        pltpu.make_async_copy(predicted, predicted_hbm, sems.at[1]),
    ]
    for copy in copies:
        copy.start()
    for copy in copies:
        copy.wait()


def deliver(predicted, update):
    vmem = pl.BlockSpec(memory_space=pltpu.VMEM)
    hbm = pl.BlockSpec(memory_space=pltpu.HBM)
    return pl.pallas_call(
        deliver_kernel,
        out_shape=(
            jax.ShapeDtypeStruct(predicted.shape, F32),
            jax.ShapeDtypeStruct(update.shape, F32),
        ),
        in_specs=[vmem, vmem],
        out_specs=(hbm, hbm),
        scratch_shapes=[pltpu.SemaphoreType.DMA((2,))],
        compiler_params=pltpu.CompilerParams(vmem_limit_bytes=2**20),
        name="deliver",
    )(predicted, update)


def body(n_facet, n_col, facets, col_offsets, sub_rows, facet_offsets, vis_pos, observed):
    assert sub_rows.shape[0] == n_facet
    n_rows = facets.shape[2]
    n_vis = vis_pos.shape[3]
    vmem = pl.BlockSpec(memory_space=pltpu.VMEM)
    facet_blocks = pltpu.VMEM((n_facet, M, 2 * M), BF16)
    col_blocks = pltpu.VMEM((n_col, n_rows, 2 * M), BF16)
    table_rows = n_col + n_facet
    vmem_left = (67043328 - 4 * (facets.size + observed.size)) // 1024 * 1024 - MARGIN
    results = pl.pallas_call(
            functools.partial(kernel, n_facet, n_col),
            out_shape=(pltpu.VMEM(observed.shape, F32), pltpu.VMEM(facets.shape, F32)),
            in_specs=[pl.BlockSpec(memory_space=pltpu.HBM)] * 6,
            out_specs=(vmem, vmem),
            scratch_shapes=[
                pltpu.VMEM((2, n_rows, YN), BF16),
                pltpu.SMEM(col_offsets.shape, jnp.int32),
                pltpu.SMEM(sub_rows.shape[::-1], jnp.int32),
                pltpu.SMEM(facet_offsets.shape[::-1], jnp.int32),
                pltpu.VMEM(vis_pos.shape, jnp.int32),
                pltpu.VMEM(observed.shape, F32),
                pltpu.VMEM((2, M, YN), F32),
                pltpu.VMEM((2, table_rows, YN), F32),
                pltpu.VMEM((n_col, 2 * M, YN), BF16),
                pltpu.VMEM((n_facet, 2 * M, YN), BF16),
                pltpu.VMEM((YN, n_facet * 2 * M), BF16),
                pltpu.VMEM((n_facet, 2 * M, n_vis), BF16),
                pltpu.VMEM((n_facet, 2 * M, n_vis), F32),
                col_blocks,
                col_blocks,
                facet_blocks,
                facet_blocks,
                facet_blocks,
                facet_blocks,
                col_blocks,
                col_blocks,
                pltpu.SemaphoreType.DMA((6,)),
                pltpu.SemaphoreType.DMA((2, n_col)),
                pltpu.SemaphoreType.DMA((2, n_col)),
                pltpu.SemaphoreType.DMA((2, n_facet)),
                pltpu.SemaphoreType.DMA((2, n_facet)),
            ],
            compiler_params=pltpu.CompilerParams(
                collective_id=0, has_side_effects=True, vmem_limit_bytes=vmem_left
            ),
            name="predict_update",
        )(facets, col_offsets, sub_rows.T, facet_offsets.T, vis_pos, observed)
    return deliver(*results)


def solution(mesh):
    in_specs = (
        P("facet", None, "col", None),
        P(),
        P(None, "col"),
        P(),
        P("facet", "col", None, None),
        P("facet", "col", None, None),
    )
    out_specs = (P("facet", "col", None, None), P("facet", None, "col", None))
    step = functools.partial(body, mesh.shape["facet"], mesh.shape["col"])
    return jax.shard_map(step, mesh=mesh, in_specs=in_specs, out_specs=out_specs, check_vma=False)
```

profile of v0, /device:TPU:0, one launch (start us, length us, event | category | flops | bytes accessed | tf_op | source)
XLA Modules:
  0.0 26.5 jit_solution(4082715772705402983)
XLA Ops:
  0.6 25.0 %predict_update.1 = (f32[1,1,2,256]{3,2,1,0:T(2,128)S(1)}, f32[1,2,96,768]{3,2,1,0:T(8,128)S(1)}) custom-call(bf16[1,2,96,768]{3,2,1,0:T(8,128)(2,1)} %facets_hbm.1, s32[8]{0:T(128)} %col_offsets_hbm.1, s32[1,4]{1,0:T(1,128)} %bitcast.3, s32[2,4]{1,0:T(2,128)} %bitcast.2, s32[1,1,2,256]{3,2,1,0:T(2,128)} %vis_pos_hbm.1, f32[1,1,2,256]{3,2,1,0:T(2,128)} %observed_hbm.1), custom_call_target="tpu_custom_call" | custom-call | tf_op jit(solution)/shard_map/predict_update/pallas_call | solution.py:329
  25.7 0.8 %deliver.1 = (f32[1,1,2,256]{3,2,1,0:T(2,128)}, f32[1,2,96,768]{3,2,1,0:T(8,128)}) custom-call(f32[1,1,2,256]{3,2,1,0:T(2,128)S(1)} %get-tuple-element.4.predicted, f32[1,2,96,768]{3,2,1,0:T(8,128)S(1)} %get-tuple-element.5.update), custom_call_target="tpu_custom_call" | custom-call | tf_op jit(solution)/shard_map/deliver/pallas_call | solution.py:306
where the time goes:
time: 26.6 us; the launch traced here: 26.5 us
  Pallas kernels  25.9 us (97%)
  between operations  0.64 us (2%)
    pallas_call x1, Pallas kernels, body(): pl.pallas_call(functools.partial(kernel, n_facet, n_col), out_shape=(pltp...  25 us
    pallas_call x1, Pallas kernels, deliver(): pl.pallas_call(deliver_kernel, out_shape=(jax.ShapeDtypeStruct(predicted....  0.84 us

commit v1 on v0

--- a/solution.py
+++ b/solution.py
@@ -13,6 +13,7 @@
 FINE = 1536
 YN = 768
 MARGIN = 8192
+PATHS_BEFORE = 2
 MESH = pl.DeviceIdType.MESH
 F32 = jnp.float32
 BF16 = jnp.bfloat16
@@ -38,6 +39,15 @@
 NN = ((1,), (0,))
 NT = ((1,), (1,))
 TN = ((0,), (0,))
+N_POWER = 7
+
+
+def cmul(a, b):
+    return a[0] * b[0] - a[1] * b[1], a[0] * b[1] + a[1] * b[0]
+
+
+def loop(n, step, carry=()):
+    return lax.fori_loop(0, n, step, carry, unroll=n <= 4)
 
 
 def kernel(
@@ -50,7 +60,8 @@
     vis_pos_hbm,
     observed_hbm,
     predicted,
-    update,
+    sides,
+    wall,
     facet_buf,
     col_offsets,
     sub_rows,
@@ -59,29 +70,35 @@
     observed,
     base,
     turn,
-    wall,
     subt,
-    subt_t,
     u_tab,
     v_tab,
     strip_out,
     strip_in,
     contrib_out,
     contrib_in,
-    back_out,
-    back_in,
-    delta_out,
-    delta_in,
+    marks,
+    points,
+    shifts,
+    powers,
+    firsts,
+    own_base,
+    own_turn,
+    paths,
+    diffs,
     load_sem,
     col_send,
     col_recv,
     facet_send,
     facet_recv,
+    diff_send,
+    diff_recv,
 ):
     my_f = lax.axis_index("facet")
     my_c = lax.axis_index("col")
     n_rows = facet_buf.shape[1]
     n_vis = vis_pos.shape[3]
+    room = paths.shape[1] // 2
 
     loads = [
         pltpu.make_async_copy(source, held, load_sem.at[i])
@@ -137,6 +154,38 @@
             device_id_type=MESH,
         )
 
+    def mark_copy(target, slot):
+        mine = marks.at[my_f, slot]
+        return pltpu.make_async_remote_copy(
+            src_ref=mine,
+            dst_ref=mine,
+            send_sem=col_send.at[1, target],
+            recv_sem=col_recv.at[1, slot],
+            device_id=(my_f, target),
+            device_id_type=MESH,
+        )
+
+    def marks_copy(target, slot):
+        return pltpu.make_async_remote_copy(
+            src_ref=marks.at[slot],
+            dst_ref=marks.at[slot],
+            send_sem=facet_send.at[1, target],
+            recv_sem=facet_recv.at[1, slot],
+            device_id=(target, my_c),
+            device_id_type=MESH,
+        )
+
+    def diff_copy(f, c, from_f, from_c):
+        mine = diffs.at[from_f, from_c]
+        return pltpu.make_async_remote_copy(
+            src_ref=mine,
+            dst_ref=mine,
+            send_sem=diff_send.at[f, c],
+            recv_sem=diff_recv.at[from_f, from_c],
+            device_id=(f, c),
+            device_id_type=MESH,
+        )
+
     base_re, base_im = cis(iota((M, YN), 0) * iota((M, YN), 1), YN, -1.0)
     inv_root = 1.0 / math.sqrt(YN)
     base[0] = base_re * inv_root
@@ -162,6 +211,12 @@
 
     def swapped(value):
         return pltpu.roll(value, M, 1)
+
+    for load in loads[3:]:
+        load.wait()
+    wide = marks.shape[3] - n_vis
+    marks[my_f, my_c, :, :n_vis] = vis_pos[0, 0, :1] + vis_pos[0, 0, 1:] * 65536
+    marks[my_f, my_c, :, n_vis:] = jnp.full((1, wide), sub_rows[0, my_f], jnp.int32)
 
     loads[2].wait()
     both = facet_buf[...]
@@ -180,6 +235,8 @@
             strip_in[c] = part
         if i == early - 1:
             pl.semaphore_wait(barrier, n_col - 1 + n_facet - 1)
+            for ready in col_order[:-1]:
+                mark_copy(ready, my_c).start()
             for ready in col_order[:early]:
                 col_copy(0, strip_out, strip_in, ready, my_c, ready).start()
         elif early <= i < n_col - 1:
@@ -187,8 +244,6 @@
 
     for s in range(n_facet):
         table(subt, n_col + s, s)
-    for load in loads[3:]:
-        load.wait()
     for tab, which in ((u_tab, 0), (v_tab, 1)):
         point = vis_pos[0, 0, pl.ds(which, 1)].astype(F32)
         low_re, low_im = cis(iota((M, n_vis), 0) * point, FINE, 1.0)
@@ -198,8 +253,15 @@
             high_re, high_im = cis(point * facet_offsets[which, f].astype(F32), FINE, 1.0)
             tab[f, :M] = (low_re * high_re - low_im * high_im).astype(tab.dtype)
             tab[f, M:] = (low_re * high_im + low_im * high_re).astype(tab.dtype)
-    for s in range(n_facet):
-        subt_t[:, 2 * M * s : 2 * M * (s + 1)] = subt[s].T
+    near_re, near_im = cis(
+        iota((M, n_rows), 0) * (iota((M, n_rows), 1) + (my_c * n_rows).astype(F32)), YN, -1.0
+    )
+    own_base[0] = near_re * inv_root
+    own_base[1] = near_im * inv_root
+    for c in col_order[:-1]:
+        mark_copy(c, c).wait_recv()
+    for f in facet_order[:-1]:
+        marks_copy(f, my_f).start()
 
     for c in col_order[:-1]:
         col_copy(0, strip_out, strip_in, c, c, c).wait_recv()
@@ -216,6 +278,77 @@
             facet_copy(0, contrib_out, contrib_in, s, my_f, s).start()
         else:
             contrib_in[s] = part
+
+    for f in facet_order[:-1]:
+        marks_copy(f, f).wait_recv()
+    sub = lax.broadcasted_iota(jnp.int32, (8, n_vis), 0)
+    bits = [lax.rem(sub // (1 << p), 2) == 1 for p in range(3)]
+    rows_at = (my_c * n_rows).astype(F32)
+
+    def spread(s, carry):
+        for c in range(n_col):
+            unit = s * n_col + c
+            points[pl.ds(unit, 1)] = marks[s, c, :, :n_vis]
+            shifts[pl.ds(unit, 1)] = marks[s, c, :, n_vis:]
+        rows = pl.ds(pl.multiple_of(s * n_col, n_col), n_col)
+        shift = shifts[rows].astype(F32) * (iota((n_col, wide), 1) + rows_at)
+        own_turn[0, rows], own_turn[1, rows] = cis(shift, YN, -1.0)
+        packed = points[rows]
+        high = packed // 65536
+        for which, point in ((0, packed - high * 65536), (1, high)):
+            point = point.astype(F32)
+            powers[which, 0, 0, rows], powers[which, 0, 1, rows] = cis(
+                point * facet_offsets[which, my_f].astype(F32), FINE, -1.0
+            )
+            value = cis(point, FINE, -1.0)
+            for p in range(1, N_POWER):
+                powers[which, p, 0, rows], powers[which, p, 1, rows] = value
+                if p < N_POWER - 1:
+                    value = cmul(value, value)
+        return carry
+
+    loop(n_facet, spread)
+
+    def power(which, p, unit):
+        return powers[which, p, 0, pl.ds(unit, 1)], powers[which, p, 1, pl.ds(unit, 1)]
+
+    def first(which, unit):
+        value = None
+        for p in range(3):
+            re, im = power(which, 1 + p, unit)
+            step = jnp.where(bits[p], re, 1.0), jnp.where(bits[p], im, 0.0)
+            value = step if value is None else cmul(value, step)
+        return cmul(value, power(which, 0, unit))
+
+    def filled(which, start, unit):
+        parts = [start]
+        for p in range(4, N_POWER):
+            by = power(which, p, unit)
+            parts += [cmul(part, by) for part in parts]
+        return [jnp.concatenate([part[i] for part in parts], axis=0) for i in range(2)]
+
+    def make_path(c):
+        def one(s, carry):
+            unit = s * n_col + c
+            u_re, u_im = filled(0, first(0, unit), unit)
+            u_re, u_im = u_re.astype(BF16), u_im.astype(BF16)
+            v_first = first(1, unit)
+            firsts[unit, 0], firsts[unit, 1] = v_first
+            re = own_turn[0, pl.ds(unit, 1), :n_rows]
+            im = own_turn[1, pl.ds(unit, 1), :n_rows]
+            e_re, e_im = cmul((own_base[0], own_base[1]), (re, im))
+            e_tab = jnp.concatenate([e_re, e_im], axis=0).astype(BF16)
+            paths[unit, :n_rows] = dot(e_tab, jnp.concatenate([u_re, u_im], axis=0), TN).astype(BF16)
+            paths[unit, room : room + n_rows] = dot(
+                e_tab, jnp.concatenate([u_im, -u_re], axis=0), TN
+            ).astype(BF16)
+            return carry
+
+        loop(n_facet, one)
+
+    near_order = col_order[::-1]
+    for c in near_order[:PATHS_BEFORE]:
+        make_path(c)
 
     pred_re = jnp.zeros((M, n_vis), F32)
     pred_im = jnp.zeros((M, n_vis), F32)
@@ -234,87 +367,102 @@
     pred_im = jnp.sum(pred_im, axis=0, keepdims=True)
     predicted[0, 0, pl.ds(0, 1)] = pred_re
     predicted[0, 0, pl.ds(1, 1)] = pred_im
-    weight = SUB / math.sqrt(n_vis)
-    diff_re = pred_re - observed[0, 0, pl.ds(0, 1)]
-    diff_im = pred_im - observed[0, 0, pl.ds(1, 1)]
-    for i, f in enumerate(facet_order):
-        v_re, v_im = v_tab[f, :M], v_tab[f, M:]
-        wgt_re = ((diff_re * v_re + diff_im * v_im) * weight).astype(BF16)
-        wgt_im = ((diff_im * v_re - diff_re * v_im) * weight).astype(BF16)
-        prod = dot(u_tab[f], jnp.concatenate([wgt_re, wgt_im], axis=0), NT)
-        part = (prod[:M] - minus_plus * swapped(prod[M:])).astype(BF16)
-        if i < n_facet - 1:
-            back_out[f] = part
-            facet_copy(1, back_out, back_in, f, my_f, f).start()
+    weight = SUB / math.sqrt(n_vis) / SUB
+    weight *= math.sqrt(YN / (M * n_facet)) * math.sqrt(YN / (M * n_col))
+    diffs[my_f, my_c] = ((predicted[0, 0] - observed[0, 0]) * weight).astype(diffs.dtype)
+    for c in col_order[:-1]:
+
+        def send(i, carry, c=c):
+            diff_copy(lax.rem(my_f + i, n_facet), c, my_f, my_c).start()
+            return carry
+
+        loop(n_facet, send)
+    for f in facet_order[:-1]:
+        diff_copy(f, my_c, my_f, my_c).start()
+
+    for c in near_order[PATHS_BEFORE:]:
+        make_path(c)
+
+    def gather(c, own):
+        def one(i, total):
+            s = lax.rem(my_f + i, n_facet)
+            unit = s * n_col + c
+            diff = diffs[s, c].astype(F32)
+            diff = diff[:1], diff[1:]
+            start = cmul((firsts[unit, 0], firsts[unit, 1]), diff)
+            wgt = jnp.concatenate(filled(1, start, unit), axis=0).astype(BF16)
+            return total + dot(paths[unit], wgt, NT)
+
+        def wait(i, carry):
+            s = lax.rem(my_f + i, n_facet)
+            diff_copy(s, c, s, c).wait_recv()
+            return carry
+
+        if own:
+            for s in facet_order[:-1]:
+                diff_copy(s, c, s, c).wait_recv()
         else:
-            back_in[f] = part
-
-    for s in facet_order[:-1]:
-        facet_copy(1, back_out, back_in, s, s, s).wait_recv()
-    stacked = []
-    for s in range(n_facet):
-        block = back_in[s]
-        stacked += [block, (-minus_plus * swapped(block.astype(F32))).astype(BF16)]
-    back_scale = math.sqrt(YN / (M * n_facet))
-    stacked = jnp.concatenate(stacked, axis=0)
-    for i, pair in enumerate(pair_order):
-        start = pl.multiple_of(pair * (2 * n_rows), 2 * n_rows)
-        delta = dot(subt_t[pl.ds(start, 2 * n_rows)], stacked, NN) * back_scale
-        delta_out[pl.ds(2 * pair, 2)] = delta.reshape(2, n_rows, 2 * M).astype(BF16)
-        for c in col_order[2 * i : 2 * i + 2]:
-            if c is not col_order[-1]:
-                col_copy(1, delta_out, delta_in, c, my_c, c).start()
-    delta_in[my_c] = delta_out[my_c]
-
-    up_scale = math.sqrt(YN / (M * n_col))
-    for i in reversed(range(n_pair)):
-        for c in col_order[2 * i : 2 * i + 2]:
-            if c is not col_order[-1]:
-                col_copy(1, delta_out, delta_in, c, c, c).wait_recv()
-        pair = pair_order[i]
-        blocks = [delta_in[2 * pair + core] for core in range(2)]
-        turned = [(-minus_plus * swapped(block.astype(F32))).astype(BF16) for block in blocks]
-        walls = wall[pl.ds(2 * pair, 2)].reshape(4 * M, YN)
-        for part, sides in enumerate((blocks, turned)):
-            term = dot(jnp.concatenate(sides, axis=1), walls, NN)
-            if i < n_pair - 1:
-                term += update[0, part]
-            update[0, part] = term * up_scale if i == 0 else term
+            loop(n_facet, wait)
+        prod = loop(n_facet, one, jnp.zeros((2 * room, 2 * M), F32))
+        re, im = prod[:n_rows], prod[room : room + n_rows]
+        at = pl.ds(pl.multiple_of(c * 2 * M, 2 * M), 2 * M)
+        sides[:n_rows, at] = (re + minus_plus * swapped(im)).astype(BF16)
+        sides[room : room + n_rows, at] = (im - minus_plus * swapped(re)).astype(BF16)
+
+    for i, c in enumerate(near_order):
+        gather(c, i == 0)
 
     for c in col_order[:-1]:
         col_copy(0, strip_out, strip_in, c, c, c).wait_send()
-        col_copy(1, delta_out, delta_in, c, c, c).wait_send()
+        mark_copy(c, my_c).wait_send()
+
+        def sent(f, carry, c=c):
+            diff_copy(f, c, my_f, my_c).wait_send()
+            return carry
+
+        loop(n_facet, sent)
     for f in facet_order[:-1]:
         facet_copy(0, contrib_out, contrib_in, f, f, f).wait_send()
-        facet_copy(1, back_out, back_in, f, f, f).wait_send()
-
-
-def deliver_kernel(predicted, update, predicted_hbm, update_hbm, sems):
-    copies = [
-        pltpu.make_async_copy(update, update_hbm, sems.at[0]),
-        pltpu.make_async_copy(predicted, predicted_hbm, sems.at[1]),
-    ]
-    for copy in copies:
-        copy.start()
+        marks_copy(f, my_f).wait_send()
+        diff_copy(f, my_c, my_f, my_c).wait_send()
+
+
+def finish_kernel(predicted, sides, wall, predicted_hbm, update_hbm, update, sems):
+    copies = [pltpu.make_async_copy(predicted, predicted_hbm, sems.at[0])]
+    copies[0].start()
+    n_rows = update.shape[1]
+    room = sides.shape[0] // 2
+    walls = wall[...].reshape(sides.shape[1], update.shape[2])
+    step = 256
+    for i in range(update.shape[2] // step):
+        at = slice(i * step, (i + 1) * step)
+        prod = dot(sides[...], walls[:, at], NN)
+        update[0, :, at] = prod[:n_rows]
+        update[1, :, at] = prod[room : room + n_rows]
+        copies.append(pltpu.make_async_copy(update.at[:, :, at], update_hbm.at[0, :, :, at], sems.at[1 + i]))
+        copies[-1].start()
     for copy in copies:
         copy.wait()
 
 
-def deliver(predicted, update):
+def finish(predicted, sides, wall, facets_shape):
     vmem = pl.BlockSpec(memory_space=pltpu.VMEM)
     hbm = pl.BlockSpec(memory_space=pltpu.HBM)
     return pl.pallas_call(
-        deliver_kernel,
+        finish_kernel,
         out_shape=(
             jax.ShapeDtypeStruct(predicted.shape, F32),
-            jax.ShapeDtypeStruct(update.shape, F32),
+            jax.ShapeDtypeStruct(facets_shape, F32),
         ),
-        in_specs=[vmem, vmem],
+        in_specs=[vmem] * 3,
         out_specs=(hbm, hbm),
-        scratch_shapes=[pltpu.SemaphoreType.DMA((2,))],
-        compiler_params=pltpu.CompilerParams(vmem_limit_bytes=2**20),
-        name="deliver",
-    )(predicted, update)
+        scratch_shapes=[
+            pltpu.VMEM(facets_shape[1:], F32),
+            pltpu.SemaphoreType.DMA((1 + facets_shape[3] // 256,)),
+        ],
+        compiler_params=pltpu.CompilerParams(vmem_limit_bytes=2**22),
+        name="finish",
+    )(predicted, sides, wall)
 
 
 def body(n_facet, n_col, facets, col_offsets, sub_rows, facet_offsets, vis_pos, observed):
@@ -325,12 +473,18 @@
     facet_blocks = pltpu.VMEM((n_facet, M, 2 * M), BF16)
     col_blocks = pltpu.VMEM((n_col, n_rows, 2 * M), BF16)
     table_rows = n_col + n_facet
-    vmem_left = (67043328 - 4 * (facets.size + observed.size)) // 1024 * 1024 - MARGIN
+    room = -(-n_rows // 16) * 16
+    wide = -(-n_rows // 128) * 128
+    n_units = n_col * n_facet
+    sides = (2 * room, n_col * 2 * M)
+    wall = (n_col, 2 * M, YN)
+    held = 4 * observed.size + 2 * (math.prod(sides) + math.prod(wall))
+    vmem_left = (67043328 - held) // 1024 * 1024 - MARGIN
     results = pl.pallas_call(
             functools.partial(kernel, n_facet, n_col),
-            out_shape=(pltpu.VMEM(observed.shape, F32), pltpu.VMEM(facets.shape, F32)),
+            out_shape=(pltpu.VMEM(observed.shape, F32), pltpu.VMEM(sides, BF16), pltpu.VMEM(wall, BF16)),
             in_specs=[pl.BlockSpec(memory_space=pltpu.HBM)] * 6,
-            out_specs=(vmem, vmem),
+            out_specs=(vmem, vmem, vmem),
             scratch_shapes=[
                 pltpu.VMEM((2, n_rows, YN), BF16),
                 pltpu.SMEM(col_offsets.shape, jnp.int32),
@@ -340,31 +494,36 @@
                 pltpu.VMEM(observed.shape, F32),
                 pltpu.VMEM((2, M, YN), F32),
                 pltpu.VMEM((2, table_rows, YN), F32),
-                pltpu.VMEM((n_col, 2 * M, YN), BF16),
                 pltpu.VMEM((n_facet, 2 * M, YN), BF16),
-                pltpu.VMEM((YN, n_facet * 2 * M), BF16),
                 pltpu.VMEM((n_facet, 2 * M, n_vis), BF16),
                 pltpu.VMEM((n_facet, 2 * M, n_vis), F32),
                 col_blocks,
                 col_blocks,
                 facet_blocks,
                 facet_blocks,
-                facet_blocks,
-                facet_blocks,
-                col_blocks,
-                col_blocks,
+                pltpu.VMEM((n_facet, n_col, 1, n_vis + wide), jnp.int32),
+                pltpu.VMEM((n_units, n_vis), jnp.int32),
+                pltpu.VMEM((n_units, wide), jnp.int32),
+                pltpu.VMEM((2, N_POWER, 2, n_units, n_vis), F32),
+                pltpu.VMEM((n_units, 2, 8, n_vis), F32),
+                pltpu.VMEM((2, M, n_rows), F32),
+                pltpu.VMEM((2, n_units, wide), F32),
+                pltpu.VMEM((n_units, 2 * room, n_vis), BF16),
+                pltpu.VMEM((n_facet, n_col, 2, n_vis), BF16),
                 pltpu.SemaphoreType.DMA((6,)),
                 pltpu.SemaphoreType.DMA((2, n_col)),
                 pltpu.SemaphoreType.DMA((2, n_col)),
                 pltpu.SemaphoreType.DMA((2, n_facet)),
                 pltpu.SemaphoreType.DMA((2, n_facet)),
+                pltpu.SemaphoreType.DMA((n_facet, n_col)),
+                pltpu.SemaphoreType.DMA((n_facet, n_col)),
             ],
             compiler_params=pltpu.CompilerParams(
                 collective_id=0, has_side_effects=True, vmem_limit_bytes=vmem_left
             ),
             name="predict_update",
         )(facets, col_offsets, sub_rows.T, facet_offsets.T, vis_pos, observed)
-    return deliver(*results)
+    return finish(*results, facets.shape)
 
 
 def solution(mesh):

time: 26.6 us -> 25.2 us (0.947)
  Pallas kernels: 25.9 us -> 24.4 us
    pallas_call x1, Pallas kernels: 25 us -> 23.1 us  [body(): pl.pallas_call(functools.partial(kernel, n_facet, n_col), out_shape=(pltp...]
    pallas_call x1, Pallas kernels: 0.84 us -> 1.25 us  [finish(): pl.pallas_call(finish_kernel, out_shape=(jax.ShapeDtypeStruct(predicted.s...]
where the time goes in v1:
time: 25.2 us; the launch traced here: 25 us
  Pallas kernels  24.4 us (97%)
  between operations  0.64 us (3%)
    pallas_call x1, Pallas kernels, body(): pl.pallas_call(functools.partial(kernel, n_facet, n_col), out_shape=(pltp...  23.1 us
    pallas_call x1, Pallas kernels, finish(): pl.pallas_call(finish_kernel, out_shape=(jax.ShapeDtypeStruct(predicted.s...  1.25 us

profile of v1, /device:TPU:0, one launch (start us, length us, event | category | flops | bytes accessed | tf_op | source)
XLA Modules:
  0.0 25.0 jit_solution(13008133907718787342)
XLA Ops:
  0.6 23.1 %predict_update.1 = (f32[1,1,2,256]{3,2,1,0:T(2,128)S(1)}, bf16[192,1024]{1,0:T(8,128)(2,1)S(1)}, bf16[8,128,768]{2,1,0:T(8,128)(2,1)S(1)}) custom-call(bf16[1,2,96,768]{3,2,1,0:T(8,128)(2,1)} %facets_hbm.1, s32[8]{0:T(128)} %col_offsets_hbm.1, s32[1,4]{1,0:T(1,128)} %bitcast.3, s32[2,4]{1,0:T(2,128)} %bitcast.2, s32[1,1,2,256]{3,2,1,0:T(2,128)} %vis_pos_hbm.1, ...), custom_call_target="tpu_custom_call" | custom-call | tf_op jit(solution)/shard_map/predict_update/pallas_call | solution.py:483
  23.7 1.3 %finish.1 = (f32[1,1,2,256]{3,2,1,0:T(2,128)}, f32[1,2,96,768]{3,2,1,0:T(8,128)}) custom-call(f32[1,1,2,256]{3,2,1,0:T(2,128)S(1)} %get-tuple-element.5.predicted, bf16[192,1024]{1,0:T(8,128)(2,1)S(1)} %get-tuple-element.6.sides, bf16[8,128,768]{2,1,0:T(8,128)(2,1)S(1)} %get-tuple-element.7.wall), custom_call_target="tpu_custom_call" | custom-call | tf_op jit(solution)/shard_map/finish/pallas_call | solution.py:451

commit v2 on v1

--- a/solution.py
+++ b/solution.py
@@ -13,7 +13,7 @@
 FINE = 1536
 YN = 768
 MARGIN = 8192
-PATHS_BEFORE = 2
+PATHS_BEFORE = 4
 MESH = pl.DeviceIdType.MESH
 F32 = jnp.float32
 BF16 = jnp.bfloat16
@@ -62,6 +62,7 @@
     predicted,
     sides,
     wall,
+    partial,
     facet_buf,
     col_offsets,
     sub_rows,
@@ -226,8 +227,9 @@
         both = both.reshape(2 * n_rows, YN)
     early = n_col - 1
     for i, c in enumerate(col_order):
-        table(wall, c, c)
-        prod = dot(both, wall[c], NT)
+        place = n_col - 1 - i
+        table(wall, c, place)
+        prod = dot(both, wall[place], NT)
         part = (prod[:n_rows] + minus_plus * swapped(prod[n_rows:])).astype(BF16)
         if i < n_col - 1:
             strip_out[c] = part
@@ -270,14 +272,13 @@
         strip = strip.astype(F32).reshape(YN, 2 * M).astype(BF16)
     else:
         strip = strip.reshape(YN, 2 * M)
-    for i, s in enumerate(facet_order):
-        prod = dot(subt[s], strip, NN)
-        part = (prod[:M] + minus_plus * swapped(prod[M:])).astype(BF16)
-        if i < n_facet - 1:
-            contrib_out[s] = part
-            facet_copy(0, contrib_out, contrib_in, s, my_f, s).start()
-        else:
-            contrib_in[s] = part
+    prods = dot(subt[...].reshape(n_facet * 2 * M, YN), strip, NN)
+    for s in range(n_facet):
+        prod = prods[s * 2 * M : (s + 1) * 2 * M]
+        contrib_out[s] = (prod[:M] + minus_plus * swapped(prod[M:])).astype(BF16)
+    for s in facet_order[:-1]:
+        facet_copy(0, contrib_out, contrib_in, s, my_f, s).start()
+    contrib_in[my_f] = contrib_out[my_f]
 
     for f in facet_order[:-1]:
         marks_copy(f, f).wait_recv()
@@ -352,10 +353,9 @@
 
     pred_re = jnp.zeros((M, n_vis), F32)
     pred_im = jnp.zeros((M, n_vis), F32)
-    for i in range(n_facet):
-        f = facet_order[n_facet - 1 - i]
-        if i > 0:
-            facet_copy(0, contrib_out, contrib_in, f, f, f).wait_recv()
+    for f in facet_order[:-1]:
+        facet_copy(0, contrib_out, contrib_in, f, f, f).wait_recv()
+    for f in range(n_facet):
         with_re = dot(contrib_in[f], u_tab[f, :M], TN)
         with_im = dot(contrib_in[f], u_tab[f, M:], TN)
         rows_re = with_re[:M] - with_im[M:]
@@ -383,7 +383,9 @@
     for c in near_order[PATHS_BEFORE:]:
         make_path(c)
 
-    def gather(c, own):
+    def gather(place):
+        c = near_order[place]
+
         def one(i, total):
             s = lax.rem(my_f + i, n_facet)
             unit = s * n_col + c
@@ -393,24 +395,33 @@
             wgt = jnp.concatenate(filled(1, start, unit), axis=0).astype(BF16)
             return total + dot(paths[unit], wgt, NT)
 
-        def wait(i, carry):
-            s = lax.rem(my_f + i, n_facet)
+        prod = loop(n_facet, one, jnp.zeros((2 * room, 2 * M), F32))
+        re, im = prod[:n_rows], prod[room : room + n_rows]
+        at = slice(place * 2 * M, (place + 1) * 2 * M)
+        sides[:n_rows, at] = (re + minus_plus * swapped(im)).astype(BF16)
+        sides[room : room + n_rows, at] = (im - minus_plus * swapped(re)).astype(BF16)
+
+    def wait_for(place):
+        c = near_order[place]
+        if place == 0:
+            for s in facet_order[:-1]:
+                diff_copy(s, c, s, c).wait_recv()
+            return
+
+        def wait(s, carry):
             diff_copy(s, c, s, c).wait_recv()
             return carry
 
-        if own:
-            for s in facet_order[:-1]:
-                diff_copy(s, c, s, c).wait_recv()
-        else:
-            loop(n_facet, wait)
-        prod = loop(n_facet, one, jnp.zeros((2 * room, 2 * M), F32))
-        re, im = prod[:n_rows], prod[room : room + n_rows]
-        at = pl.ds(pl.multiple_of(c * 2 * M, 2 * M), 2 * M)
-        sides[:n_rows, at] = (re + minus_plus * swapped(im)).astype(BF16)
-        sides[room : room + n_rows, at] = (im - minus_plus * swapped(re)).astype(BF16)
-
-    for i, c in enumerate(near_order):
-        gather(c, i == 0)
+        loop(n_facet, wait)
+
+    half = n_col // 2
+    for places in (range(half), range(half, n_col)):
+        for place in places:
+            wait_for(place)
+        for place in places:
+            gather(place)
+        if places[0] == 0:
+            partial[...] = dot(sides[:, : half * 2 * M], wall[:half].reshape(half * 2 * M, YN), NN)
 
     for c in col_order[:-1]:
         col_copy(0, strip_out, strip_in, c, c, c).wait_send()
@@ -427,16 +438,18 @@
         diff_copy(f, my_c, my_f, my_c).wait_send()
 
 
-def finish_kernel(predicted, sides, wall, predicted_hbm, update_hbm, update, sems):
+def finish_kernel(predicted, sides, wall, partial, predicted_hbm, update_hbm, update, sems):
     copies = [pltpu.make_async_copy(predicted, predicted_hbm, sems.at[0])]
     copies[0].start()
     n_rows = update.shape[1]
     room = sides.shape[0] // 2
-    walls = wall[...].reshape(sides.shape[1], update.shape[2])
+    depth = sides.shape[1] // 2
+    half = wall.shape[0] // 2
+    walls = wall[half:].reshape(depth, update.shape[2])
     step = 256
     for i in range(update.shape[2] // step):
         at = slice(i * step, (i + 1) * step)
-        prod = dot(sides[...], walls[:, at], NN)
+        prod = dot(sides[:, depth:], walls[:, at], NN) + partial[:, at]
         update[0, :, at] = prod[:n_rows]
         update[1, :, at] = prod[room : room + n_rows]
         copies.append(pltpu.make_async_copy(update.at[:, :, at], update_hbm.at[0, :, :, at], sems.at[1 + i]))
@@ -445,7 +458,7 @@
         copy.wait()
 
 
-def finish(predicted, sides, wall, facets_shape):
+def finish(predicted, sides, wall, partial, facets_shape):
     vmem = pl.BlockSpec(memory_space=pltpu.VMEM)
     hbm = pl.BlockSpec(memory_space=pltpu.HBM)
     return pl.pallas_call(
@@ -454,7 +467,7 @@
             jax.ShapeDtypeStruct(predicted.shape, F32),
             jax.ShapeDtypeStruct(facets_shape, F32),
         ),
-        in_specs=[vmem] * 3,
+        in_specs=[vmem] * 4,
         out_specs=(hbm, hbm),
         scratch_shapes=[
             pltpu.VMEM(facets_shape[1:], F32),
@@ -462,7 +475,7 @@
         ],
         compiler_params=pltpu.CompilerParams(vmem_limit_bytes=2**22),
         name="finish",
-    )(predicted, sides, wall)
+    )(predicted, sides, wall, partial)
 
 
 def body(n_facet, n_col, facets, col_offsets, sub_rows, facet_offsets, vis_pos, observed):
@@ -478,13 +491,19 @@
     n_units = n_col * n_facet
     sides = (2 * room, n_col * 2 * M)
     wall = (n_col, 2 * M, YN)
-    held = 4 * observed.size + 2 * (math.prod(sides) + math.prod(wall))
+    partial = (2 * room, YN)
+    held = 4 * (observed.size + math.prod(partial)) + 2 * (math.prod(sides) + math.prod(wall))
     vmem_left = (67043328 - held) // 1024 * 1024 - MARGIN
     results = pl.pallas_call(
             functools.partial(kernel, n_facet, n_col),
-            out_shape=(pltpu.VMEM(observed.shape, F32), pltpu.VMEM(sides, BF16), pltpu.VMEM(wall, BF16)),
+            out_shape=(
+                pltpu.VMEM(observed.shape, F32),
+                pltpu.VMEM(sides, BF16),
+                pltpu.VMEM(wall, BF16),
+                pltpu.VMEM(partial, F32),
+            ),
             in_specs=[pl.BlockSpec(memory_space=pltpu.HBM)] * 6,
-            out_specs=(vmem, vmem, vmem),
+            out_specs=(vmem, vmem, vmem, vmem),
             scratch_shapes=[
                 pltpu.VMEM((2, n_rows, YN), BF16),
                 pltpu.SMEM(col_offsets.shape, jnp.int32),

time: 25.2 us -> 23.7 us (0.940)
  Pallas kernels: 24.4 us -> 22.9 us
    pallas_call x1, Pallas kernels: 23.1 us -> 21.8 us  [body(): pl.pallas_call(functools.partial(kernel, n_facet, n_col), out_shape=(pltp...]
where the time goes in v2:
time: 23.7 us; the launch traced here: 23.6 us
  Pallas kernels  22.9 us (97%)
  between operations  0.64 us (3%)
    pallas_call x1, Pallas kernels, body(): pl.pallas_call(functools.partial(kernel, n_facet, n_col), out_shape=(pltp...  21.8 us
    pallas_call x1, Pallas kernels, finish(): pl.pallas_call(finish_kernel, out_shape=(jax.ShapeDtypeStruct(predicted.s...  1.11 us

profile of v2, /device:TPU:0, one launch (start us, length us, event | category | flops | bytes accessed | tf_op | source)
XLA Modules:
  0.0 23.6 jit_solution(15962104970384591135)
XLA Ops:
  0.6 21.8 %predict_update.1 = (f32[1,1,2,256]{3,2,1,0:T(2,128)S(1)}, bf16[192,1024]{1,0:T(8,128)(2,1)S(1)}, bf16[8,128,768]{2,1,0:T(8,128)(2,1)S(1)}, f32[192,768]{1,0:T(8,128)S(1)}) custom-call(bf16[1,2,96,768]{3,2,1,0:T(8,128)(2,1)} %facets_hbm.1, s32[8]{0:T(128)} %col_offsets_hbm.1, s32[1,4]{1,0:T(1,128)} %bitcast.3, s32[2,4]{1,0:T(2,128)} %bitcast.2, ...), custom_call_target="tpu_custom_call" | custom-call | tf_op jit(solution)/shard_map/predict_update/pallas_call | solution.py:497
  22.5 1.1 %finish.1 = (f32[1,1,2,256]{3,2,1,0:T(2,128)}, f32[1,2,96,768]{3,2,1,0:T(8,128)}) custom-call(f32[1,1,2,256]{3,2,1,0:T(2,128)S(1)} %get-tuple-element.6.predicted, bf16[192,1024]{1,0:T(8,128)(2,1)S(1)} %get-tuple-element.7.sides, bf16[8,128,768]{2,1,0:T(8,128)(2,1)S(1)} %get-tuple-element.8.wall, f32[192,768]{1,0:T(8,128)S(1)} %get-tuple-element.9.partial), custom_call_target="tpu_custom_call" | custom-call | tf_op jit(solution)/shard_map/finish/pallas_call | solution.py:464

commit v3 on v2

--- a/solution.py
+++ b/solution.py
@@ -39,6 +39,7 @@
 NN = ((1,), (0,))
 NT = ((1,), (1,))
 TN = ((0,), (0,))
+STRIP, MARK, MARKS, CONTRIB, OWN, NEAR, FAR = range(7)
 N_POWER = 7
 
 
@@ -88,12 +89,8 @@
     paths,
     diffs,
     load_sem,
-    col_send,
-    col_recv,
-    facet_send,
-    facet_recv,
-    diff_send,
-    diff_recv,
+    send_sem,
+    recv_sem,
 ):
     my_f = lax.axis_index("facet")
     my_c = lax.axis_index("col")
@@ -135,57 +132,27 @@
     for f in facet_order[:-1]:
         pl.semaphore_signal(barrier, inc=1, device_id=(f, my_c), device_id_type=MESH)
 
-    def col_copy(phase, out, into, slot_out, slot_in, target):
+    def remote(kind, source, into, f, c):
         return pltpu.make_async_remote_copy(
-            src_ref=out.at[slot_out],
-            dst_ref=into.at[slot_in],
-            send_sem=col_send.at[phase, slot_out],
-            recv_sem=col_recv.at[phase, slot_in],
-            device_id=(my_f, target),
-            device_id_type=MESH,
-        )
-
-    def facet_copy(phase, out, into, slot_out, slot_in, target):
-        return pltpu.make_async_remote_copy(
-            src_ref=out.at[slot_out],
-            dst_ref=into.at[slot_in],
-            send_sem=facet_send.at[phase, slot_out],
-            recv_sem=facet_recv.at[phase, slot_in],
-            device_id=(target, my_c),
-            device_id_type=MESH,
-        )
-
-    def mark_copy(target, slot):
-        mine = marks.at[my_f, slot]
-        return pltpu.make_async_remote_copy(
-            src_ref=mine,
-            dst_ref=mine,
-            send_sem=col_send.at[1, target],
-            recv_sem=col_recv.at[1, slot],
-            device_id=(my_f, target),
-            device_id_type=MESH,
-        )
-
-    def marks_copy(target, slot):
-        return pltpu.make_async_remote_copy(
-            src_ref=marks.at[slot],
-            dst_ref=marks.at[slot],
-            send_sem=facet_send.at[1, target],
-            recv_sem=facet_recv.at[1, slot],
-            device_id=(target, my_c),
-            device_id_type=MESH,
-        )
-
-    def diff_copy(f, c, from_f, from_c):
-        mine = diffs.at[from_f, from_c]
-        return pltpu.make_async_remote_copy(
-            src_ref=mine,
-            dst_ref=mine,
-            send_sem=diff_send.at[f, c],
-            recv_sem=diff_recv.at[from_f, from_c],
+            src_ref=source,
+            dst_ref=into,
+            send_sem=send_sem.at[kind],
+            recv_sem=recv_sem.at[kind],
             device_id=(f, c),
             device_id_type=MESH,
         )
+
+    def all_of(kind, block):
+        return remote(kind, block, block, my_f, my_c)
+
+    strips_all = all_of(STRIP, strip_in.at[: n_col - 1])
+    mark_all = all_of(MARK, marks.at[0, : n_col - 1])
+    marks_all = all_of(MARKS, marks.at[: n_facet - 1])
+    contribs_all = all_of(CONTRIB, contrib_in.at[: n_facet - 1])
+    half = n_col // 2
+    diffs_own = all_of(OWN, diffs.at[: n_facet - 1, 0])
+    diffs_near = all_of(NEAR, diffs.at[:, : half - 1])
+    diffs_far = all_of(FAR, diffs.at[:, :half])
 
     base_re, base_im = cis(iota((M, YN), 0) * iota((M, YN), 1), YN, -1.0)
     inv_root = 1.0 / math.sqrt(YN)
@@ -238,11 +205,11 @@
         if i == early - 1:
             pl.semaphore_wait(barrier, n_col - 1 + n_facet - 1)
             for ready in col_order[:-1]:
-                mark_copy(ready, my_c).start()
+                remote(MARK, marks.at[my_f, my_c], marks.at[my_f, my_c], my_f, ready).start()
             for ready in col_order[:early]:
-                col_copy(0, strip_out, strip_in, ready, my_c, ready).start()
+                remote(STRIP, strip_out.at[ready], strip_in.at[my_c], my_f, ready).start()
         elif early <= i < n_col - 1:
-            col_copy(0, strip_out, strip_in, c, my_c, c).start()
+            remote(STRIP, strip_out.at[c], strip_in.at[my_c], my_f, c).start()
 
     for s in range(n_facet):
         table(subt, n_col + s, s)
@@ -260,13 +227,11 @@
     )
     own_base[0] = near_re * inv_root
     own_base[1] = near_im * inv_root
-    for c in col_order[:-1]:
-        mark_copy(c, c).wait_recv()
+    mark_all.wait_recv()
     for f in facet_order[:-1]:
-        marks_copy(f, my_f).start()
-
-    for c in col_order[:-1]:
-        col_copy(0, strip_out, strip_in, c, c, c).wait_recv()
+        remote(MARKS, marks.at[my_f], marks.at[my_f], f, my_c).start()
+
+    strips_all.wait_recv()
     strip = strip_in[...]
     if n_rows % 16:
         strip = strip.astype(F32).reshape(YN, 2 * M).astype(BF16)
@@ -277,11 +242,10 @@
         prod = prods[s * 2 * M : (s + 1) * 2 * M]
         contrib_out[s] = (prod[:M] + minus_plus * swapped(prod[M:])).astype(BF16)
     for s in facet_order[:-1]:
-        facet_copy(0, contrib_out, contrib_in, s, my_f, s).start()
+        remote(CONTRIB, contrib_out.at[s], contrib_in.at[my_f], s, my_c).start()
     contrib_in[my_f] = contrib_out[my_f]
 
-    for f in facet_order[:-1]:
-        marks_copy(f, f).wait_recv()
+    marks_all.wait_recv()
     sub = lax.broadcasted_iota(jnp.int32, (8, n_vis), 0)
     bits = [lax.rem(sub // (1 << p), 2) == 1 for p in range(3)]
     rows_at = (my_c * n_rows).astype(F32)
@@ -353,8 +317,7 @@
 
     pred_re = jnp.zeros((M, n_vis), F32)
     pred_im = jnp.zeros((M, n_vis), F32)
-    for f in facet_order[:-1]:
-        facet_copy(0, contrib_out, contrib_in, f, f, f).wait_recv()
+    contribs_all.wait_recv()
     for f in range(n_facet):
         with_re = dot(contrib_in[f], u_tab[f, :M], TN)
         with_im = dot(contrib_in[f], u_tab[f, M:], TN)
@@ -370,15 +333,17 @@
     weight = SUB / math.sqrt(n_vis) / SUB
     weight *= math.sqrt(YN / (M * n_facet)) * math.sqrt(YN / (M * n_col))
     diffs[my_f, my_c] = ((predicted[0, 0] - observed[0, 0]) * weight).astype(diffs.dtype)
-    for c in col_order[:-1]:
-
-        def send(i, carry, c=c):
-            diff_copy(lax.rem(my_f + i, n_facet), c, my_f, my_c).start()
+    diff = diffs.at[my_f, my_c]
+    for i, c in enumerate(col_order[:-1]):
+        kind = FAR if i < half else NEAR
+
+        def send(i, carry, c=c, kind=kind):
+            remote(kind, diff, diff, lax.rem(my_f + i, n_facet), c).start()
             return carry
 
         loop(n_facet, send)
     for f in facet_order[:-1]:
-        diff_copy(f, my_c, my_f, my_c).start()
+        remote(OWN, diff, diff, f, my_c).start()
 
     for c in near_order[PATHS_BEFORE:]:
         make_path(c)
@@ -401,41 +366,17 @@
         sides[:n_rows, at] = (re + minus_plus * swapped(im)).astype(BF16)
         sides[room : room + n_rows, at] = (im - minus_plus * swapped(re)).astype(BF16)
 
-    def wait_for(place):
-        c = near_order[place]
-        if place == 0:
-            for s in facet_order[:-1]:
-                diff_copy(s, c, s, c).wait_recv()
-            return
-
-        def wait(s, carry):
-            diff_copy(s, c, s, c).wait_recv()
-            return carry
-
-        loop(n_facet, wait)
-
-    half = n_col // 2
-    for places in (range(half), range(half, n_col)):
-        for place in places:
-            wait_for(place)
-        for place in places:
-            gather(place)
-        if places[0] == 0:
-            partial[...] = dot(sides[:, : half * 2 * M], wall[:half].reshape(half * 2 * M, YN), NN)
-
-    for c in col_order[:-1]:
-        col_copy(0, strip_out, strip_in, c, c, c).wait_send()
-        mark_copy(c, my_c).wait_send()
-
-        def sent(f, carry, c=c):
-            diff_copy(f, c, my_f, my_c).wait_send()
-            return carry
-
-        loop(n_facet, sent)
-    for f in facet_order[:-1]:
-        facet_copy(0, contrib_out, contrib_in, f, f, f).wait_send()
-        marks_copy(f, my_f).wait_send()
-        diff_copy(f, my_c, my_f, my_c).wait_send()
+    diffs_own.wait_recv()
+    diffs_near.wait_recv()
+    for place in range(half):
+        gather(place)
+    partial[...] = dot(sides[:, : half * 2 * M], wall[:half].reshape(half * 2 * M, YN), NN)
+    diffs_far.wait_recv()
+    for place in range(half, n_col):
+        gather(place)
+
+    for sent in (strips_all, mark_all, marks_all, contribs_all, diffs_own, diffs_near, diffs_far):
+        sent.wait_send()
 
 
 def finish_kernel(predicted, sides, wall, partial, predicted_hbm, update_hbm, update, sems):
@@ -530,12 +471,8 @@
                 pltpu.VMEM((n_units, 2 * room, n_vis), BF16),
                 pltpu.VMEM((n_facet, n_col, 2, n_vis), BF16),
                 pltpu.SemaphoreType.DMA((6,)),
-                pltpu.SemaphoreType.DMA((2, n_col)),
-                pltpu.SemaphoreType.DMA((2, n_col)),
-                pltpu.SemaphoreType.DMA((2, n_facet)),
-                pltpu.SemaphoreType.DMA((2, n_facet)),
-                pltpu.SemaphoreType.DMA((n_facet, n_col)),
-                pltpu.SemaphoreType.DMA((n_facet, n_col)),
+                pltpu.SemaphoreType.DMA((7,)),
+                pltpu.SemaphoreType.DMA((7,)),
             ],
             compiler_params=pltpu.CompilerParams(
                 collective_id=0, has_side_effects=True, vmem_limit_bytes=vmem_left

time: 23.7 us -> 22.8 us (0.962)
  Pallas kernels: 22.9 us -> 22 us
    pallas_call x1, Pallas kernels: 21.8 us -> 20.9 us  [body(): pl.pallas_call(functools.partial(kernel, n_facet, n_col), out_shape=(pltp...]
where the time goes in v3:
time: 22.8 us; the launch traced here: 22.6 us
  Pallas kernels  22 us (96%)
  between operations  0.64 us (3%)
    pallas_call x1, Pallas kernels, body(): pl.pallas_call(functools.partial(kernel, n_facet, n_col), out_shape=(pltp...  20.9 us
    pallas_call x1, Pallas kernels, finish(): pl.pallas_call(finish_kernel, out_shape=(jax.ShapeDtypeStruct(predicted.s...  1.1 us

profile of v3, /device:TPU:0, one launch (start us, length us, event | category | flops | bytes accessed | tf_op | source)
XLA Modules:
  0.0 22.6 jit_solution(10827693541191207821)
XLA Ops:
  0.6 20.9 %predict_update.1 = (f32[1,1,2,256]{3,2,1,0:T(2,128)S(1)}, bf16[192,1024]{1,0:T(8,128)(2,1)S(1)}, bf16[8,128,768]{2,1,0:T(8,128)(2,1)S(1)}, f32[192,768]{1,0:T(8,128)S(1)}) custom-call(bf16[1,2,96,768]{3,2,1,0:T(8,128)(2,1)} %facets_hbm.1, s32[8]{0:T(128)} %col_offsets_hbm.1, s32[1,4]{1,0:T(1,128)} %bitcast.3, s32[2,4]{1,0:T(2,128)} %bitcast.2, ...), custom_call_target="tpu_custom_call" | custom-call | tf_op jit(solution)/shard_map/predict_update/pallas_call | solution.py:438
  21.5 1.1 %finish.1 = (f32[1,1,2,256]{3,2,1,0:T(2,128)}, f32[1,2,96,768]{3,2,1,0:T(8,128)}) custom-call(f32[1,1,2,256]{3,2,1,0:T(2,128)S(1)} %get-tuple-element.6.predicted, bf16[192,1024]{1,0:T(8,128)(2,1)S(1)} %get-tuple-element.7.sides, bf16[8,128,768]{2,1,0:T(8,128)(2,1)S(1)} %get-tuple-element.8.wall, f32[192,768]{1,0:T(8,128)S(1)} %get-tuple-element.9.partial), custom_call_target="tpu_custom_call" | custom-call | tf_op jit(solution)/shard_map/finish/pallas_call | solution.py:405

commit v4 on v3

--- a/solution.py
+++ b/solution.py
@@ -13,7 +13,6 @@
 FINE = 1536
 YN = 768
 MARGIN = 8192
-PATHS_BEFORE = 4
 MESH = pl.DeviceIdType.MESH
 F32 = jnp.float32
 BF16 = jnp.bfloat16
@@ -39,7 +38,7 @@
 NN = ((1,), (0,))
 NT = ((1,), (1,))
 TN = ((0,), (0,))
-STRIP, MARK, MARKS, CONTRIB, OWN, NEAR, FAR = range(7)
+STRIP, MARK, MARKS, PEER, MEASURED, SEEN, NEAR, FAR = range(8)
 N_POWER = 7
 
 
@@ -77,8 +76,10 @@
     v_tab,
     strip_out,
     strip_in,
-    contrib_out,
-    contrib_in,
+    seen_out,
+    seen_in,
+    peers,
+    measured,
     marks,
     points,
     shifts,
@@ -126,7 +127,12 @@
     col_order = []
     for pair in pair_order:
         col_order += [2 * pair + 1 - my_core, 2 * pair + my_core]
-    facet_order = [lax.rem(my_f + 1 + i, n_facet) for i in range(n_facet)]
+    bits = n_facet.bit_length() - 1
+    assert n_facet == 1 << bits
+    facet_order = []
+    for i in range(n_facet - 1, -1, -1):
+        turns = [(i >> b & 1) * (1 << b) * (1 - 2 * lax.rem(my_f // (1 << b), 2)) for b in range(bits)]
+        facet_order.append(my_f + sum(turns))
     for c in col_order[:-1]:
         pl.semaphore_signal(barrier, inc=1, device_id=(my_f, c), device_id_type=MESH)
     for f in facet_order[:-1]:
@@ -148,11 +154,12 @@
     strips_all = all_of(STRIP, strip_in.at[: n_col - 1])
     mark_all = all_of(MARK, marks.at[0, : n_col - 1])
     marks_all = all_of(MARKS, marks.at[: n_facet - 1])
-    contribs_all = all_of(CONTRIB, contrib_in.at[: n_facet - 1])
+    peers_all = all_of(PEER, peers.at[: n_facet - 1])
+    seen_all = all_of(SEEN, seen_in.at[: n_facet - 1])
     half = n_col // 2
-    diffs_own = all_of(OWN, diffs.at[: n_facet - 1, 0])
-    diffs_near = all_of(NEAR, diffs.at[:, : half - 1])
-    diffs_far = all_of(FAR, diffs.at[:, :half])
+    measured_all = all_of(MEASURED, measured.at[: n_facet - 1])
+    diffs_near = all_of(NEAR, diffs.at[: half - 1])
+    diffs_far = all_of(FAR, diffs.at[:half])
 
     base_re, base_im = cis(iota((M, YN), 0) * iota((M, YN), 1), YN, -1.0)
     inv_root = 1.0 / math.sqrt(YN)
@@ -183,7 +190,10 @@
     for load in loads[3:]:
         load.wait()
     wide = marks.shape[3] - n_vis
-    marks[my_f, my_c, :, :n_vis] = vis_pos[0, 0, :1] + vis_pos[0, 0, 1:] * 65536
+    own_points = vis_pos[0, 0, :1] + vis_pos[0, 0, 1:] * 65536
+    peers[my_f] = own_points
+    measured[my_f] = observed[0, 0]
+    marks[my_f, my_c, :, :n_vis] = own_points
     marks[my_f, my_c, :, n_vis:] = jnp.full((1, wide), sub_rows[0, my_f], jnp.int32)
 
     loads[2].wait()
@@ -192,7 +202,7 @@
         both = both.astype(F32).reshape(2 * n_rows, YN).astype(BF16)
     else:
         both = both.reshape(2 * n_rows, YN)
-    early = n_col - 1
+    early = 2
     for i, c in enumerate(col_order):
         place = n_col - 1 - i
         table(wall, c, place)
@@ -206,6 +216,9 @@
             pl.semaphore_wait(barrier, n_col - 1 + n_facet - 1)
             for ready in col_order[:-1]:
                 remote(MARK, marks.at[my_f, my_c], marks.at[my_f, my_c], my_f, ready).start()
+            for f in facet_order[:-1]:
+                remote(PEER, peers.at[my_f], peers.at[my_f], f, my_c).start()
+                remote(MEASURED, measured.at[my_f], measured.at[my_f], f, my_c).start()
             for ready in col_order[:early]:
                 remote(STRIP, strip_out.at[ready], strip_in.at[my_c], my_f, ready).start()
         elif early <= i < n_col - 1:
@@ -213,20 +226,26 @@
 
     for s in range(n_facet):
         table(subt, n_col + s, s)
-    for tab, which in ((u_tab, 0), (v_tab, 1)):
-        point = vis_pos[0, 0, pl.ds(which, 1)].astype(F32)
-        low_re, low_im = cis(iota((M, n_vis), 0) * point, FINE, 1.0)
-        low_re = low_re * (1.0 / math.sqrt(SUB))
-        low_im = low_im * (1.0 / math.sqrt(SUB))
-        for f in range(n_facet):
-            high_re, high_im = cis(point * facet_offsets[which, f].astype(F32), FINE, 1.0)
-            tab[f, :M] = (low_re * high_re - low_im * high_im).astype(tab.dtype)
-            tab[f, M:] = (low_re * high_im + low_im * high_re).astype(tab.dtype)
     near_re, near_im = cis(
         iota((M, n_rows), 0) * (iota((M, n_rows), 1) + (my_c * n_rows).astype(F32)), YN, -1.0
     )
     own_base[0] = near_re * inv_root
     own_base[1] = near_im * inv_root
+    def unpack(packed):
+        high = packed // 65536
+        return packed - high * 65536, high
+
+    peers_all.wait_recv()
+
+    def make_tables(s, carry):
+        for tab, which, point in zip((u_tab, v_tab), range(2), unpack(peers[s])):
+            at = iota((M, n_vis), 0) + facet_offsets[which, my_f].astype(F32)
+            re, im = cis(at * point.astype(F32), FINE, 1.0)
+            tab[s, :M] = (re * (1.0 / math.sqrt(SUB))).astype(tab.dtype)
+            tab[s, M:] = (im * (1.0 / math.sqrt(SUB))).astype(tab.dtype)
+        return carry
+
+    loop(n_facet, make_tables)
     mark_all.wait_recv()
     for f in facet_order[:-1]:
         remote(MARKS, marks.at[my_f], marks.at[my_f], f, my_c).start()
@@ -240,14 +259,21 @@
     prods = dot(subt[...].reshape(n_facet * 2 * M, YN), strip, NN)
     for s in range(n_facet):
         prod = prods[s * 2 * M : (s + 1) * 2 * M]
-        contrib_out[s] = (prod[:M] + minus_plus * swapped(prod[M:])).astype(BF16)
-    for s in facet_order[:-1]:
-        remote(CONTRIB, contrib_out.at[s], contrib_in.at[my_f], s, my_c).start()
-    contrib_in[my_f] = contrib_out[my_f]
+        part = (prod[:M] + minus_plus * swapped(prod[M:])).astype(BF16)
+        with_re = dot(part, u_tab[s, :M], TN)
+        with_im = dot(part, u_tab[s, M:], TN)
+        rows_re = with_re[:M] - with_im[M:]
+        rows_im = with_im[:M] + with_re[M:]
+        v_re, v_im = v_tab[s, :M], v_tab[s, M:]
+        seen_out[s, :1] = jnp.sum(rows_re * v_re - rows_im * v_im, axis=0, keepdims=True)
+        seen_out[s, 1:] = jnp.sum(rows_re * v_im + rows_im * v_re, axis=0, keepdims=True)
+    for f in facet_order[:-1]:
+        remote(SEEN, seen_out, seen_in.at[my_f], f, my_c).start()
+    seen_in[my_f] = seen_out[...]
 
     marks_all.wait_recv()
     sub = lax.broadcasted_iota(jnp.int32, (8, n_vis), 0)
-    bits = [lax.rem(sub // (1 << p), 2) == 1 for p in range(3)]
+    odd = [lax.rem(sub // (1 << p), 2) == 1 for p in range(3)]
     rows_at = (my_c * n_rows).astype(F32)
 
     def spread(s, carry):
@@ -259,8 +285,7 @@
         shift = shifts[rows].astype(F32) * (iota((n_col, wide), 1) + rows_at)
         own_turn[0, rows], own_turn[1, rows] = cis(shift, YN, -1.0)
         packed = points[rows]
-        high = packed // 65536
-        for which, point in ((0, packed - high * 65536), (1, high)):
+        for which, point in enumerate(unpack(packed)):
             point = point.astype(F32)
             powers[which, 0, 0, rows], powers[which, 0, 1, rows] = cis(
                 point * facet_offsets[which, my_f].astype(F32), FINE, -1.0
@@ -281,7 +306,7 @@
         value = None
         for p in range(3):
             re, im = power(which, 1 + p, unit)
-            step = jnp.where(bits[p], re, 1.0), jnp.where(bits[p], im, 0.0)
+            step = jnp.where(odd[p], re, 1.0), jnp.where(odd[p], im, 0.0)
             value = step if value is None else cmul(value, step)
         return cmul(value, power(which, 0, unit))
 
@@ -312,40 +337,25 @@
         loop(n_facet, one)
 
     near_order = col_order[::-1]
-    for c in near_order[:PATHS_BEFORE]:
+    for c in near_order[:6]:
         make_path(c)
 
-    pred_re = jnp.zeros((M, n_vis), F32)
-    pred_im = jnp.zeros((M, n_vis), F32)
-    contribs_all.wait_recv()
-    for f in range(n_facet):
-        with_re = dot(contrib_in[f], u_tab[f, :M], TN)
-        with_im = dot(contrib_in[f], u_tab[f, M:], TN)
-        rows_re = with_re[:M] - with_im[M:]
-        rows_im = with_im[:M] + with_re[M:]
-        v_re, v_im = v_tab[f, :M], v_tab[f, M:]
-        pred_re += rows_re * v_re - rows_im * v_im
-        pred_im += rows_re * v_im + rows_im * v_re
-    pred_re = jnp.sum(pred_re, axis=0, keepdims=True)
-    pred_im = jnp.sum(pred_im, axis=0, keepdims=True)
-    predicted[0, 0, pl.ds(0, 1)] = pred_re
-    predicted[0, 0, pl.ds(1, 1)] = pred_im
+    seen_all.wait_recv()
+    measured_all.wait_recv()
     weight = SUB / math.sqrt(n_vis) / SUB
     weight *= math.sqrt(YN / (M * n_facet)) * math.sqrt(YN / (M * n_col))
-    diffs[my_f, my_c] = ((predicted[0, 0] - observed[0, 0]) * weight).astype(diffs.dtype)
-    diff = diffs.at[my_f, my_c]
+    pred = seen_in[0]
+    for f in range(1, n_facet):
+        pred += seen_in[f]
+    diffs[my_c] = ((pred - measured[...]) * weight).astype(diffs.dtype)
     for i, c in enumerate(col_order[:-1]):
-        kind = FAR if i < half else NEAR
-
-        def send(i, carry, c=c, kind=kind):
-            remote(kind, diff, diff, lax.rem(my_f + i, n_facet), c).start()
-            return carry
-
-        loop(n_facet, send)
-    for f in facet_order[:-1]:
-        remote(OWN, diff, diff, f, my_c).start()
-
-    for c in near_order[PATHS_BEFORE:]:
+        remote(FAR if i < half else NEAR, diffs.at[my_c], diffs.at[my_c], my_f, c).start()
+    mine = seen_in[0, my_f]
+    for f in range(1, n_facet):
+        mine += seen_in[f, my_f]
+    predicted[0, 0] = mine
+
+    for c in near_order[6:]:
         make_path(c)
 
     def gather(place):
@@ -354,7 +364,7 @@
         def one(i, total):
             s = lax.rem(my_f + i, n_facet)
             unit = s * n_col + c
-            diff = diffs[s, c].astype(F32)
+            diff = diffs[c, s].astype(F32)
             diff = diff[:1], diff[1:]
             start = cmul((firsts[unit, 0], firsts[unit, 1]), diff)
             wgt = jnp.concatenate(filled(1, start, unit), axis=0).astype(BF16)
@@ -366,7 +376,6 @@
         sides[:n_rows, at] = (re + minus_plus * swapped(im)).astype(BF16)
         sides[room : room + n_rows, at] = (im - minus_plus * swapped(re)).astype(BF16)
 
-    diffs_own.wait_recv()
     diffs_near.wait_recv()
     for place in range(half):
         gather(place)
@@ -375,7 +384,7 @@
     for place in range(half, n_col):
         gather(place)
 
-    for sent in (strips_all, mark_all, marks_all, contribs_all, diffs_own, diffs_near, diffs_far):
+    for sent in (strips_all, mark_all, marks_all, peers_all, measured_all, seen_all, diffs_near, diffs_far):
         sent.wait_send()
 
 
@@ -424,7 +433,6 @@
     n_rows = facets.shape[2]
     n_vis = vis_pos.shape[3]
     vmem = pl.BlockSpec(memory_space=pltpu.VMEM)
-    facet_blocks = pltpu.VMEM((n_facet, M, 2 * M), BF16)
     col_blocks = pltpu.VMEM((n_col, n_rows, 2 * M), BF16)
     table_rows = n_col + n_facet
     room = -(-n_rows // 16) * 16
@@ -459,8 +467,10 @@
                 pltpu.VMEM((n_facet, 2 * M, n_vis), F32),
                 col_blocks,
                 col_blocks,
-                facet_blocks,
-                facet_blocks,
+                pltpu.VMEM((n_facet, 2, n_vis), F32),
+                pltpu.VMEM((n_facet, n_facet, 2, n_vis), F32),
+                pltpu.VMEM((n_facet, 1, n_vis), jnp.int32),
+                pltpu.VMEM((n_facet, 2, n_vis), F32),
                 pltpu.VMEM((n_facet, n_col, 1, n_vis + wide), jnp.int32),
                 pltpu.VMEM((n_units, n_vis), jnp.int32),
                 pltpu.VMEM((n_units, wide), jnp.int32),
@@ -469,10 +479,10 @@
                 pltpu.VMEM((2, M, n_rows), F32),
                 pltpu.VMEM((2, n_units, wide), F32),
                 pltpu.VMEM((n_units, 2 * room, n_vis), BF16),
-                pltpu.VMEM((n_facet, n_col, 2, n_vis), BF16),
+                pltpu.VMEM((n_col, n_facet, 2, n_vis), BF16),
                 pltpu.SemaphoreType.DMA((6,)),
-                pltpu.SemaphoreType.DMA((7,)),
-                pltpu.SemaphoreType.DMA((7,)),
+                pltpu.SemaphoreType.DMA((8,)),
+                pltpu.SemaphoreType.DMA((8,)),
             ],
             compiler_params=pltpu.CompilerParams(
                 collective_id=0, has_side_effects=True, vmem_limit_bytes=vmem_left

time: 22.8 us -> 22.4 us (0.982)
  Pallas kernels: 22 us -> 21.7 us
    pallas_call x1, Pallas kernels: 20.9 us -> 20.6 us  [body(): pl.pallas_call(functools.partial(kernel, n_facet, n_col), out_shape=(pltp...]
where the time goes in v4:
time: 22.4 us; the launch traced here: 22.3 us
  Pallas kernels  21.7 us (97%)
  between operations  0.64 us (3%)
    pallas_call x1, Pallas kernels, body(): pl.pallas_call(functools.partial(kernel, n_facet, n_col), out_shape=(pltp...  20.6 us
    pallas_call x1, Pallas kernels, finish(): pl.pallas_call(finish_kernel, out_shape=(jax.ShapeDtypeStruct(predicted.s...  1.1 us

profile of v4, /device:TPU:0, one launch (start us, length us, event | category | flops | bytes accessed | tf_op | source)
XLA Modules:
  0.0 22.3 jit_solution(8121303006836888406)
XLA Ops:
  0.6 20.6 %predict_update.1 = (f32[1,1,2,256]{3,2,1,0:T(2,128)S(1)}, bf16[192,1024]{1,0:T(8,128)(2,1)S(1)}, bf16[8,128,768]{2,1,0:T(8,128)(2,1)S(1)}, f32[192,768]{1,0:T(8,128)S(1)}) custom-call(bf16[1,2,96,768]{3,2,1,0:T(8,128)(2,1)} %facets_hbm.1, s32[8]{0:T(128)} %col_offsets_hbm.1, s32[1,4]{1,0:T(1,128)} %bitcast.3, s32[2,4]{1,0:T(2,128)} %bitcast.2, ...), custom_call_target="tpu_custom_call" | custom-call | tf_op jit(solution)/shard_map/predict_update/pallas_call | solution.py:446
  21.2 1.1 %finish.1 = (f32[1,1,2,256]{3,2,1,0:T(2,128)}, f32[1,2,96,768]{3,2,1,0:T(8,128)}) custom-call(f32[1,1,2,256]{3,2,1,0:T(2,128)S(1)} %get-tuple-element.6.predicted, bf16[192,1024]{1,0:T(8,128)(2,1)S(1)} %get-tuple-element.7.sides, bf16[8,128,768]{2,1,0:T(8,128)(2,1)S(1)} %get-tuple-element.8.wall, f32[192,768]{1,0:T(8,128)S(1)} %get-tuple-element.9.partial), custom_call_target="tpu_custom_call" | custom-call | tf_op jit(solution)/shard_map/finish/pallas_call | solution.py:414

commit v5 on v4

--- a/solution.py
+++ b/solution.py
@@ -38,7 +38,7 @@
 NN = ((1,), (0,))
 NT = ((1,), (1,))
 TN = ((0,), (0,))
-STRIP, MARK, MARKS, PEER, MEASURED, SEEN, NEAR, FAR = range(8)
+STRIP, MARK, MARKS, PEER, MEASURED, SEEN, NEAR, FAR, ANSWER = range(9)
 N_POWER = 7
 
 
@@ -80,6 +80,7 @@
     seen_in,
     peers,
     measured,
+    answer,
     marks,
     points,
     shifts,
@@ -155,10 +156,10 @@
     mark_all = all_of(MARK, marks.at[0, : n_col - 1])
     marks_all = all_of(MARKS, marks.at[: n_facet - 1])
     peers_all = all_of(PEER, peers.at[: n_facet - 1])
-    seen_all = all_of(SEEN, seen_in.at[: n_facet - 1])
+    gate = 2 * my_pair + 1
+    at_gate = my_core == 1
+    seat = my_core * n_facet + my_f
     half = n_col // 2
-    measured_all = all_of(MEASURED, measured.at[: n_facet - 1])
-    diffs_near = all_of(NEAR, diffs.at[: half - 1])
     diffs_far = all_of(FAR, diffs.at[:half])
 
     base_re, base_im = cis(iota((M, YN), 0) * iota((M, YN), 1), YN, -1.0)
@@ -192,7 +193,7 @@
     wide = marks.shape[3] - n_vis
     own_points = vis_pos[0, 0, :1] + vis_pos[0, 0, 1:] * 65536
     peers[my_f] = own_points
-    measured[my_f] = observed[0, 0]
+    measured[seat] = observed[0, 0]
     marks[my_f, my_c, :, :n_vis] = own_points
     marks[my_f, my_c, :, n_vis:] = jnp.full((1, wide), sub_rows[0, my_f], jnp.int32)
 
@@ -218,7 +219,6 @@
                 remote(MARK, marks.at[my_f, my_c], marks.at[my_f, my_c], my_f, ready).start()
             for f in facet_order[:-1]:
                 remote(PEER, peers.at[my_f], peers.at[my_f], f, my_c).start()
-                remote(MEASURED, measured.at[my_f], measured.at[my_f], f, my_c).start()
             for ready in col_order[:early]:
                 remote(STRIP, strip_out.at[ready], strip_in.at[my_c], my_f, ready).start()
         elif early <= i < n_col - 1:
@@ -236,6 +236,16 @@
         return packed - high * 65536, high
 
     peers_all.wait_recv()
+
+    def to_gates(kind, source, into):
+        for f in facet_order[:-1]:
+            remote(kind, source, into, f, gate).start()
+
+        @pl.when(my_core == 0)
+        def _():
+            remote(kind, source, into, my_f, gate).start()
+
+    to_gates(MEASURED, measured.at[seat], measured.at[seat])
 
     def make_tables(s, carry):
         for tab, which, point in zip((u_tab, v_tab), range(2), unpack(peers[s])):
@@ -267,9 +277,11 @@
         v_re, v_im = v_tab[s, :M], v_tab[s, M:]
         seen_out[s, :1] = jnp.sum(rows_re * v_re - rows_im * v_im, axis=0, keepdims=True)
         seen_out[s, 1:] = jnp.sum(rows_re * v_im + rows_im * v_re, axis=0, keepdims=True)
-    for f in facet_order[:-1]:
-        remote(SEEN, seen_out, seen_in.at[my_f], f, my_c).start()
-    seen_in[my_f] = seen_out[...]
+    to_gates(SEEN, seen_out, seen_in.at[seat])
+
+    @pl.when(at_gate)
+    def _():
+        seen_in[seat] = seen_out[...]
 
     marks_all.wait_recv()
     sub = lax.broadcasted_iota(jnp.int32, (8, n_vis), 0)
@@ -340,20 +352,30 @@
     for c in near_order[:6]:
         make_path(c)
 
-    seen_all.wait_recv()
-    measured_all.wait_recv()
     weight = SUB / math.sqrt(n_vis) / SUB
     weight *= math.sqrt(YN / (M * n_facet)) * math.sqrt(YN / (M * n_col))
-    pred = seen_in[0]
-    for f in range(1, n_facet):
-        pred += seen_in[f]
-    diffs[my_c] = ((pred - measured[...]) * weight).astype(diffs.dtype)
-    for i, c in enumerate(col_order[:-1]):
-        remote(FAR if i < half else NEAR, diffs.at[my_c], diffs.at[my_c], my_f, c).start()
-    mine = seen_in[0, my_f]
-    for f in range(1, n_facet):
-        mine += seen_in[f, my_f]
-    predicted[0, 0] = mine
+
+    @pl.when(at_gate)
+    def _():
+        all_of(MEASURED, measured.at[: 2 * n_facet - 1]).wait_recv()
+        all_of(SEEN, seen_in.at[: 2 * n_facet - 1]).wait_recv()
+        for core in range(2):
+            first = core * n_facet
+            pred = seen_in[first]
+            for f in range(1, n_facet):
+                pred += seen_in[first + f]
+            diff = (pred - measured[first : first + n_facet]) * weight
+            diffs[2 * my_pair + core] = diff.astype(diffs.dtype)
+        block = diffs.at[pl.ds(2 * my_pair, 2)]
+        for i, c in enumerate(col_order[:-1]):
+            remote(FAR if i < half else NEAR, block, block, my_f, c).start()
+        for core in range(2):
+            mine = seen_in[core * n_facet, my_f]
+            for f in range(1, n_facet):
+                mine += seen_in[core * n_facet + f, my_f]
+            answer[core] = mine
+        remote(ANSWER, answer.at[0], answer.at[0], my_f, 2 * my_pair).start()
+        predicted[0, 0] = answer[1]
 
     for c in near_order[6:]:
         make_path(c)
@@ -376,7 +398,14 @@
         sides[:n_rows, at] = (re + minus_plus * swapped(im)).astype(BF16)
         sides[room : room + n_rows, at] = (im - minus_plus * swapped(re)).astype(BF16)
 
-    diffs_near.wait_recv()
+    @pl.when(at_gate)
+    def _():
+        all_of(NEAR, diffs.at[: half - 2]).wait_recv()
+
+    @pl.when(my_core == 0)
+    def _():
+        all_of(NEAR, diffs.at[:half]).wait_recv()
+
     for place in range(half):
         gather(place)
     partial[...] = dot(sides[:, : half * 2 * M], wall[:half].reshape(half * 2 * M, YN), NN)
@@ -384,8 +413,23 @@
     for place in range(half, n_col):
         gather(place)
 
-    for sent in (strips_all, mark_all, marks_all, peers_all, measured_all, seen_all, diffs_near, diffs_far):
+    for sent in (strips_all, mark_all, marks_all, peers_all):
         sent.wait_send()
+
+    @pl.when(at_gate)
+    def _():
+        all_of(MEASURED, measured.at[: n_facet - 1]).wait_send()
+        all_of(SEEN, seen_in.at[: n_facet - 1]).wait_send()
+        all_of(FAR, diffs).wait_send()
+        all_of(NEAR, diffs.at[: n_col - 2]).wait_send()
+        all_of(ANSWER, answer.at[0]).wait_send()
+
+    @pl.when(my_core == 0)
+    def _():
+        all_of(MEASURED, measured.at[:n_facet]).wait_send()
+        all_of(SEEN, seen_in.at[:n_facet]).wait_send()
+        all_of(ANSWER, answer.at[0]).wait_recv()
+        predicted[0, 0] = answer[0]
 
 
 def finish_kernel(predicted, sides, wall, partial, predicted_hbm, update_hbm, update, sems):
@@ -468,9 +512,10 @@
                 col_blocks,
                 col_blocks,
                 pltpu.VMEM((n_facet, 2, n_vis), F32),
-                pltpu.VMEM((n_facet, n_facet, 2, n_vis), F32),
+                pltpu.VMEM((2 * n_facet, n_facet, 2, n_vis), F32),
                 pltpu.VMEM((n_facet, 1, n_vis), jnp.int32),
-                pltpu.VMEM((n_facet, 2, n_vis), F32),
+                pltpu.VMEM((2 * n_facet, 2, n_vis), F32),
+                pltpu.VMEM((2, 2, n_vis), F32),
                 pltpu.VMEM((n_facet, n_col, 1, n_vis + wide), jnp.int32),
                 pltpu.VMEM((n_units, n_vis), jnp.int32),
                 pltpu.VMEM((n_units, wide), jnp.int32),
@@ -481,8 +526,8 @@
                 pltpu.VMEM((n_units, 2 * room, n_vis), BF16),
                 pltpu.VMEM((n_col, n_facet, 2, n_vis), BF16),
                 pltpu.SemaphoreType.DMA((6,)),
-                pltpu.SemaphoreType.DMA((8,)),
-                pltpu.SemaphoreType.DMA((8,)),
+                pltpu.SemaphoreType.DMA((9,)),
+                pltpu.SemaphoreType.DMA((9,)),
             ],
             compiler_params=pltpu.CompilerParams(
                 collective_id=0, has_side_effects=True, vmem_limit_bytes=vmem_left

time: 22.4 us -> 21.6 us (0.964)
  Pallas kernels: 21.7 us -> 20.8 us
    pallas_call x1, Pallas kernels: 20.6 us -> 19.7 us  [body(): pl.pallas_call(functools.partial(kernel, n_facet, n_col), out_shape=(pltp...]
where the time goes in v5:
time: 21.6 us; the launch traced here: 21.4 us
  Pallas kernels  20.8 us (96%)
  between operations  0.64 us (3%)
    pallas_call x1, Pallas kernels, body(): pl.pallas_call(functools.partial(kernel, n_facet, n_col), out_shape=(pltp...  19.7 us
    pallas_call x1, Pallas kernels, finish(): pl.pallas_call(finish_kernel, out_shape=(jax.ShapeDtypeStruct(predicted.s...  1.1 us

profile of v5, /device:TPU:0, one launch (start us, length us, event | category | flops | bytes accessed | tf_op | source)
XLA Modules:
  0.0 21.4 jit_solution(5015354722132029482)
XLA Ops:
  0.6 19.7 %predict_update.1 = (f32[1,1,2,256]{3,2,1,0:T(2,128)S(1)}, bf16[192,1024]{1,0:T(8,128)(2,1)S(1)}, bf16[8,128,768]{2,1,0:T(8,128)(2,1)S(1)}, f32[192,768]{1,0:T(8,128)S(1)}) custom-call(bf16[1,2,96,768]{3,2,1,0:T(8,128)(2,1)} %facets_hbm.1, s32[8]{0:T(128)} %col_offsets_hbm.1, s32[1,4]{1,0:T(1,128)} %bitcast.3, s32[2,4]{1,0:T(2,128)} %bitcast.2, ...), custom_call_target="tpu_custom_call" | custom-call | tf_op jit(solution)/shard_map/predict_update/pallas_call | solution.py:490
  20.3 1.1 %finish.1 = (f32[1,1,2,256]{3,2,1,0:T(2,128)}, f32[1,2,96,768]{3,2,1,0:T(8,128)}) custom-call(f32[1,1,2,256]{3,2,1,0:T(2,128)S(1)} %get-tuple-element.6.predicted, bf16[192,1024]{1,0:T(8,128)(2,1)S(1)} %get-tuple-element.7.sides, bf16[8,128,768]{2,1,0:T(8,128)(2,1)S(1)} %get-tuple-element.8.wall, f32[192,768]{1,0:T(8,128)S(1)} %get-tuple-element.9.partial), custom_call_target="tpu_custom_call" | custom-call | tf_op jit(solution)/shard_map/finish/pallas_call | solution.py:458

commit v6 on v5

--- a/solution.py
+++ b/solution.py
@@ -38,7 +38,7 @@
 NN = ((1,), (0,))
 NT = ((1,), (1,))
 TN = ((0,), (0,))
-STRIP, MARK, MARKS, PEER, MEASURED, SEEN, NEAR, FAR, ANSWER = range(9)
+STRIP, CLOSE, MARK, MARKS, PEER, MEASURED, SEEN, NEAR, FAR, ANSWER = range(10)
 N_POWER = 7
 
 
@@ -76,6 +76,7 @@
     v_tab,
     strip_out,
     strip_in,
+    near_prods,
     seen_out,
     seen_in,
     peers,
@@ -126,8 +127,9 @@
         pair_order.append(target + side * (n_pair - 1 - 2 * target))
     pair_order.append(my_pair)
     col_order = []
-    for pair in pair_order:
-        col_order += [2 * pair + 1 - my_core, 2 * pair + my_core]
+    for pair in pair_order[:-1]:
+        col_order += [2 * pair, 2 * pair + 1]
+    col_order += [2 * my_pair + 1 - my_core, my_c]
     bits = n_facet.bit_length() - 1
     assert n_facet == 1 << bits
     facet_order = []
@@ -152,7 +154,6 @@
     def all_of(kind, block):
         return remote(kind, block, block, my_f, my_c)
 
-    strips_all = all_of(STRIP, strip_in.at[: n_col - 1])
     mark_all = all_of(MARK, marks.at[0, : n_col - 1])
     marks_all = all_of(MARKS, marks.at[: n_facet - 1])
     peers_all = all_of(PEER, peers.at[: n_facet - 1])
@@ -160,6 +161,10 @@
     at_gate = my_core == 1
     seat = my_core * n_facet + my_f
     half = n_col // 2
+    strips_far = all_of(STRIP, strip_in.at[:half])
+    strips_near = all_of(CLOSE, strip_in.at[: half - 1])
+    near_start = side * half
+    far_start = half - near_start
     diffs_far = all_of(FAR, diffs.at[:half])
 
     base_re, base_im = cis(iota((M, YN), 0) * iota((M, YN), 1), YN, -1.0)
@@ -203,7 +208,7 @@
         both = both.astype(F32).reshape(2 * n_rows, YN).astype(BF16)
     else:
         both = both.reshape(2 * n_rows, YN)
-    early = 2
+    early = half
     for i, c in enumerate(col_order):
         place = n_col - 1 - i
         table(wall, c, place)
@@ -222,7 +227,8 @@
             for ready in col_order[:early]:
                 remote(STRIP, strip_out.at[ready], strip_in.at[my_c], my_f, ready).start()
         elif early <= i < n_col - 1:
-            remote(STRIP, strip_out.at[c], strip_in.at[my_c], my_f, c).start()
+            kind = STRIP if i < half else CLOSE
+            remote(kind, strip_out.at[c], strip_in.at[my_c], my_f, c).start()
 
     for s in range(n_facet):
         table(subt, n_col + s, s)
@@ -260,13 +266,21 @@
     for f in facet_order[:-1]:
         remote(MARKS, marks.at[my_f], marks.at[my_f], f, my_c).start()
 
-    strips_all.wait_recv()
-    strip = strip_in[...]
-    if n_rows % 16:
-        strip = strip.astype(F32).reshape(YN, 2 * M).astype(BF16)
-    else:
-        strip = strip.reshape(YN, 2 * M)
-    prods = dot(subt[...].reshape(n_facet * 2 * M, YN), strip, NN)
+    depth = half * n_rows
+
+    def contribute(start):
+        strip = strip_in[pl.ds(start, half)]
+        if n_rows % 16:
+            strip = strip.astype(F32).reshape(depth, 2 * M).astype(BF16)
+        else:
+            strip = strip.reshape(depth, 2 * M)
+        part = subt[:, :, pl.ds(pl.multiple_of(start * n_rows, depth), depth)]
+        return dot(part.reshape(n_facet * 2 * M, depth), strip, NN)
+
+    strips_near.wait_recv()
+    near_prods[...] = contribute(near_start)
+    strips_far.wait_recv()
+    prods = contribute(far_start) + near_prods[...]
     for s in range(n_facet):
         prod = prods[s * 2 * M : (s + 1) * 2 * M]
         part = (prod[:M] + minus_plus * swapped(prod[M:])).astype(BF16)
@@ -413,7 +427,7 @@
     for place in range(half, n_col):
         gather(place)
 
-    for sent in (strips_all, mark_all, marks_all, peers_all):
+    for sent in (strips_far, strips_near, mark_all, marks_all, peers_all):
         sent.wait_send()
 
     @pl.when(at_gate)
@@ -511,6 +525,7 @@
                 pltpu.VMEM((n_facet, 2 * M, n_vis), F32),
                 col_blocks,
                 col_blocks,
+                pltpu.VMEM((n_facet * 2 * M, 2 * M), F32),
                 pltpu.VMEM((n_facet, 2, n_vis), F32),
                 pltpu.VMEM((2 * n_facet, n_facet, 2, n_vis), F32),
                 pltpu.VMEM((n_facet, 1, n_vis), jnp.int32),
@@ -526,8 +541,8 @@
                 pltpu.VMEM((n_units, 2 * room, n_vis), BF16),
                 pltpu.VMEM((n_col, n_facet, 2, n_vis), BF16),
                 pltpu.SemaphoreType.DMA((6,)),
-                pltpu.SemaphoreType.DMA((9,)),
-                pltpu.SemaphoreType.DMA((9,)),
+                pltpu.SemaphoreType.DMA((10,)),
+                pltpu.SemaphoreType.DMA((10,)),
             ],
             compiler_params=pltpu.CompilerParams(
                 collective_id=0, has_side_effects=True, vmem_limit_bytes=vmem_left

time: 21.6 us -> 21 us (0.972)
  Pallas kernels: 20.8 us -> 20.2 us
    pallas_call x1, Pallas kernels: 19.7 us -> 19.1 us  [body(): pl.pallas_call(functools.partial(kernel, n_facet, n_col), out_shape=(pltp...]
where the time goes in v6:
time: 21 us; the launch traced here: 20.9 us
  Pallas kernels  20.2 us (96%)
  between operations  0.64 us (3%)
    pallas_call x1, Pallas kernels, body(): pl.pallas_call(functools.partial(kernel, n_facet, n_col), out_shape=(pltp...  19.1 us
    pallas_call x1, Pallas kernels, finish(): pl.pallas_call(finish_kernel, out_shape=(jax.ShapeDtypeStruct(predicted.s...  1.1 us

profile of v6, /device:TPU:0, one launch (start us, length us, event | category | flops | bytes accessed | tf_op | source)
XLA Modules:
  0.0 20.9 jit_solution(2139421703527045070)
XLA Ops:
  0.6 19.1 %predict_update.1 = (f32[1,1,2,256]{3,2,1,0:T(2,128)S(1)}, bf16[192,1024]{1,0:T(8,128)(2,1)S(1)}, bf16[8,128,768]{2,1,0:T(8,128)(2,1)S(1)}, f32[192,768]{1,0:T(8,128)S(1)}) custom-call(bf16[1,2,96,768]{3,2,1,0:T(8,128)(2,1)} %facets_hbm.1, s32[8]{0:T(128)} %col_offsets_hbm.1, s32[1,4]{1,0:T(1,128)} %bitcast.3, s32[2,4]{1,0:T(2,128)} %bitcast.2, ...), custom_call_target="tpu_custom_call" | custom-call | tf_op jit(solution)/shard_map/predict_update/pallas_call | solution.py:504
  19.8 1.1 %finish.1 = (f32[1,1,2,256]{3,2,1,0:T(2,128)}, f32[1,2,96,768]{3,2,1,0:T(8,128)}) custom-call(f32[1,1,2,256]{3,2,1,0:T(2,128)S(1)} %get-tuple-element.6.predicted, bf16[192,1024]{1,0:T(8,128)(2,1)S(1)} %get-tuple-element.7.sides, bf16[8,128,768]{2,1,0:T(8,128)(2,1)S(1)} %get-tuple-element.8.wall, f32[192,768]{1,0:T(8,128)S(1)} %get-tuple-element.9.partial), custom_call_target="tpu_custom_call" | custom-call | tf_op jit(solution)/shard_map/finish/pallas_call | solution.py:472

commit v7 on v6

--- a/solution.py
+++ b/solution.py
@@ -114,8 +114,6 @@
             )
         )
     ]
-    for load in loads:
-        load.start()
     barrier = pltpu.get_barrier_semaphore()
     n_pair = n_col // 2
     my_pair, my_core = my_c // 2, lax.rem(my_c, 2)
@@ -140,6 +138,8 @@
         pl.semaphore_signal(barrier, inc=1, device_id=(my_f, c), device_id_type=MESH)
     for f in facet_order[:-1]:
         pl.semaphore_signal(barrier, inc=1, device_id=(f, my_c), device_id_type=MESH)
+    for load in loads:
+        load.start()
 
     def remote(kind, source, into, f, c):
         return pltpu.make_async_remote_copy(
@@ -220,12 +220,14 @@
             strip_in[c] = part
         if i == early - 1:
             pl.semaphore_wait(barrier, n_col - 1 + n_facet - 1)
-            for ready in col_order[:-1]:
+            for ready in col_order[:half]:
                 remote(MARK, marks.at[my_f, my_c], marks.at[my_f, my_c], my_f, ready).start()
+            for ready in col_order[:early]:
+                remote(STRIP, strip_out.at[ready], strip_in.at[my_c], my_f, ready).start()
             for f in facet_order[:-1]:
                 remote(PEER, peers.at[my_f], peers.at[my_f], f, my_c).start()
-            for ready in col_order[:early]:
-                remote(STRIP, strip_out.at[ready], strip_in.at[my_c], my_f, ready).start()
+            for ready in col_order[half:-1]:
+                remote(MARK, marks.at[my_f, my_c], marks.at[my_f, my_c], my_f, ready).start()
         elif early <= i < n_col - 1:
             kind = STRIP if i < half else CLOSE
             remote(kind, strip_out.at[c], strip_in.at[my_c], my_f, c).start()
@@ -363,7 +365,7 @@
         loop(n_facet, one)
 
     near_order = col_order[::-1]
-    for c in near_order[:6]:
+    for c in near_order[:4]:
         make_path(c)
 
     weight = SUB / math.sqrt(n_vis) / SUB
@@ -391,22 +393,21 @@
         remote(ANSWER, answer.at[0], answer.at[0], my_f, 2 * my_pair).start()
         predicted[0, 0] = answer[1]
 
-    for c in near_order[6:]:
+    for c in near_order[4:]:
         make_path(c)
 
     def gather(place):
         c = near_order[place]
 
-        def one(i, total):
-            s = lax.rem(my_f + i, n_facet)
+        def one(s):
             unit = s * n_col + c
             diff = diffs[c, s].astype(F32)
             diff = diff[:1], diff[1:]
             start = cmul((firsts[unit, 0], firsts[unit, 1]), diff)
             wgt = jnp.concatenate(filled(1, start, unit), axis=0).astype(BF16)
-            return total + dot(paths[unit], wgt, NT)
-
-        prod = loop(n_facet, one, jnp.zeros((2 * room, 2 * M), F32))
+            return dot(paths[unit], wgt, NT)
+
+        prod = lax.fori_loop(1, n_facet, lambda s, total: total + one(s), one(0), unroll=n_facet <= 4)
         re, im = prod[:n_rows], prod[room : room + n_rows]
         at = slice(place * 2 * M, (place + 1) * 2 * M)
         sides[:n_rows, at] = (re + minus_plus * swapped(im)).astype(BF16)

time: 21 us -> 21 us (level)
  no operation moved by 1% of the time
where the time goes in v7:
time: 21 us; the launch traced here: 20.9 us
  Pallas kernels  20.2 us (96%)
  between operations  0.64 us (3%)
    pallas_call x1, Pallas kernels, body(): pl.pallas_call(functools.partial(kernel, n_facet, n_col), out_shape=(pltp...  19.1 us
    pallas_call x1, Pallas kernels, finish(): pl.pallas_call(finish_kernel, out_shape=(jax.ShapeDtypeStruct(predicted.s...  1.1 us

profile of v7, /device:TPU:0, one launch (start us, length us, event | category | flops | bytes accessed | tf_op | source)
XLA Modules:
  0.0 20.9 jit_solution(11262488268137999097)
XLA Ops:
  0.6 19.1 %predict_update.1 = (f32[1,1,2,256]{3,2,1,0:T(2,128)S(1)}, bf16[192,1024]{1,0:T(8,128)(2,1)S(1)}, bf16[8,128,768]{2,1,0:T(8,128)(2,1)S(1)}, f32[192,768]{1,0:T(8,128)S(1)}) custom-call(bf16[1,2,96,768]{3,2,1,0:T(8,128)(2,1)} %facets_hbm.1, s32[8]{0:T(128)} %col_offsets_hbm.1, s32[1,4]{1,0:T(1,128)} %bitcast.3, s32[2,4]{1,0:T(2,128)} %bitcast.2, ...), custom_call_target="tpu_custom_call" | custom-call | tf_op jit(solution)/shard_map/predict_update/pallas_call | solution.py:505
  19.8 1.1 %finish.1 = (f32[1,1,2,256]{3,2,1,0:T(2,128)}, f32[1,2,96,768]{3,2,1,0:T(8,128)}) custom-call(f32[1,1,2,256]{3,2,1,0:T(2,128)S(1)} %get-tuple-element.6.predicted, bf16[192,1024]{1,0:T(8,128)(2,1)S(1)} %get-tuple-element.7.sides, bf16[8,128,768]{2,1,0:T(8,128)(2,1)S(1)} %get-tuple-element.8.wall, f32[192,768]{1,0:T(8,128)S(1)} %get-tuple-element.9.partial), custom_call_target="tpu_custom_call" | custom-call | tf_op jit(solution)/shard_map/finish/pallas_call | solution.py:473

commit v8 on v7

--- a/solution.py
+++ b/solution.py
@@ -38,7 +38,7 @@
 NN = ((1,), (0,))
 NT = ((1,), (1,))
 TN = ((0,), (0,))
-STRIP, CLOSE, MARK, MARKS, PEER, MEASURED, SEEN, NEAR, FAR, ANSWER = range(10)
+STRIP, CLOSE, MARK, MARKS, PEER, MEASURED, SEEN, MINE, NEAR, FAR, ANSWER = range(11)
 N_POWER = 7
 
 
@@ -384,7 +384,7 @@
             diffs[2 * my_pair + core] = diff.astype(diffs.dtype)
         block = diffs.at[pl.ds(2 * my_pair, 2)]
         for i, c in enumerate(col_order[:-1]):
-            remote(FAR if i < half else NEAR, block, block, my_f, c).start()
+            remote(FAR if i < half else NEAR if i < n_col - 2 else MINE, block, block, my_f, c).start()
         for core in range(2):
             mine = seen_in[core * n_facet, my_f]
             for f in range(1, n_facet):
@@ -413,16 +413,16 @@
         sides[:n_rows, at] = (re + minus_plus * swapped(im)).astype(BF16)
         sides[room : room + n_rows, at] = (im - minus_plus * swapped(re)).astype(BF16)
 
-    @pl.when(at_gate)
-    def _():
-        all_of(NEAR, diffs.at[: half - 2]).wait_recv()
-
     @pl.when(my_core == 0)
     def _():
-        all_of(NEAR, diffs.at[:half]).wait_recv()
-
-    for place in range(half):
-        gather(place)
+        all_of(MINE, diffs.at[:2]).wait_recv()
+
+    for step in range(2):
+        gather(step)
+    diffs_near = all_of(NEAR, diffs.at[: half - 2])
+    diffs_near.wait_recv()
+    for step in range(2, half):
+        gather(step)
     partial[...] = dot(sides[:, : half * 2 * M], wall[:half].reshape(half * 2 * M, YN), NN)
     diffs_far.wait_recv()
     for place in range(half, n_col):
@@ -436,7 +436,8 @@
         all_of(MEASURED, measured.at[: n_facet - 1]).wait_send()
         all_of(SEEN, seen_in.at[: n_facet - 1]).wait_send()
         all_of(FAR, diffs).wait_send()
-        all_of(NEAR, diffs.at[: n_col - 2]).wait_send()
+        all_of(NEAR, diffs.at[: n_col - 4]).wait_send()
+        all_of(MINE, diffs.at[:2]).wait_send()
         all_of(ANSWER, answer.at[0]).wait_send()
 
     @pl.when(my_core == 0)
@@ -542,8 +543,8 @@
                 pltpu.VMEM((n_units, 2 * room, n_vis), BF16),
                 pltpu.VMEM((n_col, n_facet, 2, n_vis), BF16),
                 pltpu.SemaphoreType.DMA((6,)),
-                pltpu.SemaphoreType.DMA((10,)),
-                pltpu.SemaphoreType.DMA((10,)),
+                pltpu.SemaphoreType.DMA((11,)),
+                pltpu.SemaphoreType.DMA((11,)),
             ],
             compiler_params=pltpu.CompilerParams(
                 collective_id=0, has_side_effects=True, vmem_limit_bytes=vmem_left

time: 21 us -> 21 us (level)
  no operation moved by 1% of the time
where the time goes in v8:
time: 21 us; the launch traced here: 20.9 us
  Pallas kernels  20.2 us (96%)
  between operations  0.64 us (3%)
    pallas_call x1, Pallas kernels, body(): pl.pallas_call(functools.partial(kernel, n_facet, n_col), out_shape=(pltp...  19.1 us
    pallas_call x1, Pallas kernels, finish(): pl.pallas_call(finish_kernel, out_shape=(jax.ShapeDtypeStruct(predicted.s...  1.1 us

profile of v8, /device:TPU:0, one launch (start us, length us, event | category | flops | bytes accessed | tf_op | source)
XLA Modules:
  0.0 20.9 jit_solution(15729196283632074857)
XLA Ops:
  0.6 19.1 %predict_update.1 = (f32[1,1,2,256]{3,2,1,0:T(2,128)S(1)}, bf16[192,1024]{1,0:T(8,128)(2,1)S(1)}, bf16[8,128,768]{2,1,0:T(8,128)(2,1)S(1)}, f32[192,768]{1,0:T(8,128)S(1)}) custom-call(bf16[1,2,96,768]{3,2,1,0:T(8,128)(2,1)} %facets_hbm.1, s32[8]{0:T(128)} %col_offsets_hbm.1, s32[1,4]{1,0:T(1,128)} %bitcast.3, s32[2,4]{1,0:T(2,128)} %bitcast.2, ...), custom_call_target="tpu_custom_call" | custom-call | tf_op jit(solution)/shard_map/predict_update/pallas_call | solution.py:506
  19.8 1.1 %finish.1 = (f32[1,1,2,256]{3,2,1,0:T(2,128)}, f32[1,2,96,768]{3,2,1,0:T(8,128)}) custom-call(f32[1,1,2,256]{3,2,1,0:T(2,128)S(1)} %get-tuple-element.6.predicted, bf16[192,1024]{1,0:T(8,128)(2,1)S(1)} %get-tuple-element.7.sides, bf16[8,128,768]{2,1,0:T(8,128)(2,1)S(1)} %get-tuple-element.8.wall, f32[192,768]{1,0:T(8,128)S(1)} %get-tuple-element.9.partial), custom_call_target="tpu_custom_call" | custom-call | tf_op jit(solution)/shard_map/finish/pallas_call | solution.py:474

commit v9 on v7

--- a/solution.py
+++ b/solution.py
@@ -208,7 +208,7 @@
         both = both.astype(F32).reshape(2 * n_rows, YN).astype(BF16)
     else:
         both = both.reshape(2 * n_rows, YN)
-    early = half
+    early = half - 1
     for i, c in enumerate(col_order):
         place = n_col - 1 - i
         table(wall, c, place)

time: 21 us -> 21 us (level)
  no operation moved by 1% of the time
where the time goes in v9:
time: 21 us; the launch traced here: 20.9 us
  Pallas kernels  20.2 us (96%)
  between operations  0.64 us (3%)
    pallas_call x1, Pallas kernels, body(): pl.pallas_call(functools.partial(kernel, n_facet, n_col), out_shape=(pltp...  19.1 us
    pallas_call x1, Pallas kernels, finish(): pl.pallas_call(finish_kernel, out_shape=(jax.ShapeDtypeStruct(predicted.s...  1.1 us

profile of v9, /device:TPU:0, one launch (start us, length us, event | category | flops | bytes accessed | tf_op | source)
XLA Modules:
  0.0 20.9 jit_solution(16079310580664988722)
XLA Ops:
  0.6 19.1 %predict_update.1 = (f32[1,1,2,256]{3,2,1,0:T(2,128)S(1)}, bf16[192,1024]{1,0:T(8,128)(2,1)S(1)}, bf16[8,128,768]{2,1,0:T(8,128)(2,1)S(1)}, f32[192,768]{1,0:T(8,128)S(1)}) custom-call(bf16[1,2,96,768]{3,2,1,0:T(8,128)(2,1)} %facets_hbm.1, s32[8]{0:T(128)} %col_offsets_hbm.1, s32[1,4]{1,0:T(1,128)} %bitcast.3, s32[2,4]{1,0:T(2,128)} %bitcast.2, ...), custom_call_target="tpu_custom_call" | custom-call | tf_op jit(solution)/shard_map/predict_update/pallas_call | solution.py:505
  19.8 1.1 %finish.1 = (f32[1,1,2,256]{3,2,1,0:T(2,128)}, f32[1,2,96,768]{3,2,1,0:T(8,128)}) custom-call(f32[1,1,2,256]{3,2,1,0:T(2,128)S(1)} %get-tuple-element.6.predicted, bf16[192,1024]{1,0:T(8,128)(2,1)S(1)} %get-tuple-element.7.sides, bf16[8,128,768]{2,1,0:T(8,128)(2,1)S(1)} %get-tuple-element.8.wall, f32[192,768]{1,0:T(8,128)S(1)} %get-tuple-element.9.partial), custom_call_target="tpu_custom_call" | custom-call | tf_op jit(solution)/shard_map/finish/pallas_call | solution.py:473
